TPU v7x, 32 devices: a whole 2x2x4 slice. The times are simulated.
32 devices in a mesh: row: 4 (over z), col: 4 (over y, x), layer: 2 (over core).
Axes of the slice: x: 2, y: 2, z: 4, core: 2. Of those that a mesh axis runs over, the one named last changes fastest.
Arguments:
- wavefunction: float32 [4096, 4096], P('row', 'col'), may hold values from -0.015625 to 1.515625
- start_block: float32 [4096, 2048], P(('col', 'layer'), 'row'), may hold values from -6 to 6
Outputs:
- basis: float32 [4096, 2048], P(('col', 'layer'), 'row')
All inputs are finite; a program needn't handle non-finite values.
Results may differ from a plain program's by a relative error of at most 0.0003.
Values sent between devices are 32-bit elements; how exact they have to be, the bound alone decides.
No kernel may reach another device: no remote copies, remote signals or barrier semaphores. Data moves between devices by JAX's collectives and lax.ppermute only.
A program may use at most 128 MiB of HBM per device.

v0:
```python
import functools, math
import jax, jax.numpy as jnp
from jax import lax
from jax.experimental import pallas as pl
from jax.experimental.pallas import tpu as pltpu
from jax.sharding import PartitionSpec as P

F32, BF16 = jnp.float32, jnp.bfloat16
NN = (((1,), (0,)), ((), ()))
NT = (((1,), (1,)), ((), ()))
TN = (((0,), (0,)), ((), ()))
STEPS = 5


def mm(a, b, dims):
    return lax.dot_general(a, b, dims, preferred_element_type=F32)


def split(x):
    high = x.astype(BF16)
    return high, (x - high.astype(F32)).astype(BF16)


def mm3(a, b, dims):
    return mm(a[0], b[0], dims) + (mm(a[0], b[1], dims) + mm(a[1], b[0], dims))


def iotas(n):
    return lax.broadcasted_iota(jnp.int32, (n, n), 0), lax.broadcasted_iota(jnp.int32, (n, n), 1)


def lower_half(x, rows, cols):
    return jnp.where(rows > cols, x, jnp.where(rows == cols, 0.5 * x, 0.0))


def inverse_factor(block, out_ref, work_ref):
    n = block.shape[0]
    rows, cols = iotas(n)
    eye = (rows == cols).astype(F32)
    on_diag = block * eye
    scale_row = lax.rsqrt(jnp.sum(on_diag, axis=0, keepdims=True))
    scale_col = lax.rsqrt(jnp.sum(on_diag, axis=1, keepdims=True))
    scaled = block * scale_row * scale_col
    w = scaled
    half = lower_half(w - eye, rows, cols)
    x = eye - half
    hb = half.astype(BF16)
    w = w - mm(hb, w.astype(BF16), NN)
    w = w - mm(w.astype(BF16), hb, NT)
    for _ in range(STEPS - 1):
        hb = lower_half(w - eye, rows, cols).astype(BF16)
        x = x - mm(hb, x.astype(BF16), NN)
        w = w - mm(hb, w.astype(BF16), NN)
        w = w - mm(w.astype(BF16), hb, NT)
    xs = split(x)
    error = mm3(split(mm3(xs, split(scaled), NN)), xs, NT) - eye
    x = x - mm3(split(lower_half(error, rows, cols)), xs, NN)
    out_ref[...] = x * scale_row
    size = jnp.sum(error * error)

    @pl.when(jnp.logical_not(size < 1e-3))
    def _():
        work_ref[...] = block
        out_ref[...] = eye

        @pl.loop(0, n)
        def _(j):
            state = work_ref[...]
            factors = out_ref[...]
            column = jnp.sum(jnp.where(cols == j, state, 0.0), axis=1, keepdims=True)
            below = lax.broadcasted_iota(jnp.int32, (n, 1), 0)
            pivot = jnp.sum(jnp.where(below == j, column, 0.0), axis=0, keepdims=True)
            multiplier = jnp.where(below > j, column / pivot, 0.0)
            work_ref[...] = state - multiplier * work_ref[pl.ds(j, 1), :]
            out_ref[...] = factors - multiplier * out_ref[pl.ds(j, 1), :]

        pivots = jnp.sum(work_ref[...] * eye, axis=1, keepdims=True)
        out_ref[...] = out_ref[...] * lax.rsqrt(pivots)


def factor_kernel(blocks, size, groups, bundles, shares, swaps, scale, me_ref, order_ref, *refs):
    per = blocks // groups
    width = per * size
    arrays = shares + swaps
    g_refs = [refs[n * arrays:(n + 1) * arrays] for n in range(len(bundles))]
    refs = refs[len(bundles) * arrays:]
    b_refs = [refs[s * per:(s + 1) * per] for s in range(groups)]
    out_ref, g, b, left3, right3, x_ref, work_ref, sem = refs[groups * per:]
    me = me_ref[0]
    pieces = shares * (1 + swaps)
    copies = [[] for _ in range(groups)]
    n_sem = 0
    for bundle, arrays_in in zip(bundles, g_refs):
        for t in range(pieces):
            piece = arrays_in[t] if t < shares else arrays_in[shares + t // shares - 1].at[t % shares]
            first = 0
            for s in bundle:
                rows = (s + 1) * width // pieces
                start = pl.multiple_of((me - s) * width + order_ref[t] * rows, 8)
                for h in range(per):
                    copies[s].append(pltpu.make_async_copy(
                        piece.at[pl.ds(first, rows), pl.ds(h * size, size)],
                        g.at[(me - s) * per + h, pl.ds(start, rows), :], sem.at[n_sem]))
                    n_sem += 1
                first += rows
    for s in range(groups):
        for h in range(per):
            copies[s].append(pltpu.make_async_copy(b_refs[s][h], b.at[(me - s) * per + h], sem.at[n_sem]))
            n_sem += 1

    def each_group(wanted, act):
        for s in range(groups):
            @pl.when(wanted(s))
            def _():
                for c in copies[s]:
                    act(c)

    each_group(lambda s: s == me, lambda c: c.start())
    each_group(lambda s: s < me, lambda c: c.start())
    each_group(lambda s: s == me, lambda c: c.wait())
    count = (me + 1) * per

    def rows_of(i):
        return pl.ds(pl.multiple_of(i * size, size), size)

    @pl.loop(0, count)
    def _(k):
        inverse_factor(g[k, rows_of(k), :], x_ref, work_ref)
        xs = split(x_ref[...])

        @pl.when(k == 0)
        def _():
            each_group(lambda s: s < me, lambda c: c.wait())

        done = mm3(split(b[k]), xs, NT)
        high, low = split(done)
        done3 = jnp.concatenate([high, high, low], axis=1)

        @pl.when(k >= me * per)
        def _():
            out_ref[:, pl.ds(pl.multiple_of((k - me * per) * size, size), size)] = done * scale

        @pl.loop(k + 1, count)
        def _(i):
            hi, lo = split(mm3(split(g[k, rows_of(i), :]), xs, NT))
            left3[i] = jnp.concatenate([hi, hi, lo], axis=1)
            right3[i] = jnp.concatenate([hi, lo, hi], axis=1)

        @pl.loop(k + 1, count)
        def _(j):
            right = right3[j]
            b[j] = b[j] - mm(done3, right, NT)

            @pl.loop(j, count)
            def _(i):
                g[j, rows_of(i), :] = g[j, rows_of(i), :] - mm(left3[i], right, NT)


def factor_apply(me, order, bundles, g_arrays, shares, b_groups, size, scale):
    groups, per = len(b_groups), len(b_groups[0])
    swaps = len(g_arrays[0]) - shares
    rows = b_groups[0][0].shape[0]
    blocks = groups * per
    any_spec = pl.BlockSpec(memory_space=pl.ANY)
    smem = pl.BlockSpec(memory_space=pltpu.SMEM)
    arrays = sum(g_arrays, []) + sum(b_groups, [])
    return pl.pallas_call(
        functools.partial(factor_kernel, blocks, size, groups, bundles, shares, swaps, scale),
        out_shape=jax.ShapeDtypeStruct((rows, per * size), F32),
        in_specs=[smem, smem] + [any_spec] * len(arrays),
        out_specs=pl.BlockSpec(memory_space=pltpu.VMEM),
        scratch_shapes=[
            pltpu.VMEM((blocks, blocks * size, size), F32),
            pltpu.VMEM((blocks, rows, size), F32),
            pltpu.VMEM((blocks, size, 3 * size), BF16),
            pltpu.VMEM((blocks, size, 3 * size), BF16),
            pltpu.VMEM((size, size), F32),
            pltpu.VMEM((size, size), F32),
            pltpu.SemaphoreType.DMA((groups * per * (shares * (1 + swaps) + 1),)),
        ],
        compiler_params=pltpu.CompilerParams(vmem_limit_bytes=56 * 1024 * 1024),
        cost_estimate=pl.CostEstimate(flops=6 * 10**10, bytes_accessed=2 * 10**7, transcendentals=0),
        name="factor",
    )(me, order, *arrays)


def image_call(places, s_places, blocks, starts, sizes, per, inner=None):
    last = inner is not None
    rows_n, cols_n, layers = sizes
    cut, wide = blocks[0][0].shape
    cuts = len(blocks[0])
    rows_s, panel = starts[0].shape
    any_spec = pl.BlockSpec(memory_space=pl.ANY)
    smem = pl.BlockSpec(memory_space=pltpu.SMEM)
    vmem = pl.BlockSpec(memory_space=pltpu.VMEM)
    scratch = [
        pltpu.VMEM((rows_n, cuts * cut, wide), F32),
        pltpu.VMEM((rows_n * layers, rows_s, panel), F32),
        pltpu.SemaphoreType.DMA((len(blocks) * cuts + len(starts),)),
    ]
    flat = sum(blocks, [])
    if last:
        shape = [jax.ShapeDtypeStruct((cols_n, rows_s, panel // per), F32)] * (per * layers)
        spec = [any_spec] * (per * layers)
        scratch += [
            pltpu.VMEM((wide, panel), F32),
            pltpu.VMEM((rows_n, layers, rows_s, panel), F32),
            pltpu.SemaphoreType.DMA((rows_n, layers, per)),
        ]
        flops = 6 * wide * panel * cuts * cut * (rows_n + 1)
    else:
        shape, spec = jax.ShapeDtypeStruct((wide, panel), F32), vmem
        flops = 6 * wide * panel * cuts * cut * (rows_n - 1)
    return pl.pallas_call(
        functools.partial(image_kernel, sizes, cuts, per, last),
        out_shape=shape,
        in_specs=[smem, smem] + [any_spec] * (len(flat) + len(starts)) + [vmem] * last,
        out_specs=spec,
        scratch_shapes=scratch,
        compiler_params=pltpu.CompilerParams(vmem_limit_bytes=56 * 1024 * 1024),
        cost_estimate=pl.CostEstimate(flops=flops, bytes_accessed=4 * cuts * cut * wide * rows_n, transcendentals=0),
        name="image" if last else "inner",
    )(places, s_places, *flat, *starts, *([inner] if last else []))


def image_kernel(sizes, cuts, per, last, place_ref, s_place_ref, *refs):
    rows_n, cols_n, layers = sizes
    far = rows_n - 1
    hops = [0]
    for step in range(1, rows_n if last else far):
        hops += [-step, step]
    n_a, shares = len(hops) * cuts, cols_n * layers
    a_refs, s_refs, refs = refs[:n_a], refs[n_a:n_a + shares], refs[n_a + shares:]
    if last:
        outs = refs[1:1 + per * layers]
        a, s, sem, acc, o, out_sem = refs[1 + per * layers:]
    else:
        acc, a, s, sem = refs
    me, col, layer = place_ref[0], place_ref[1], place_ref[2]
    cut = a_refs[0].shape[0]
    rows_s, panel = s_refs[0].shape
    size = panel // per

    def each_block(z, act):
        for n in range(n_a):
            @pl.when(me + hops[n // cuts] == z)
            def _():
                act(pltpu.make_async_copy(
                    a_refs[n], a.at[z, pl.ds(n % cuts * cut, cut), :], sem.at[n]))

    def each_share(z, act):
        for n in range(shares):
            @pl.when(s_place_ref[n] // layers == z)
            def _():
                act(pltpu.make_async_copy(s_refs[n], s.at[s_place_ref[n]], sem.at[n_a + n]))

    def rows_of(m):
        return pl.ds(pl.multiple_of(m * rows_s, rows_s), rows_s)

    def add_product(z):
        each_block(z, lambda c: c.wait())
        each_share(z, lambda c: c.wait())

        @pl.loop(0, layers)
        def _(m):
            acc[...] += mm3(split(a[z, rows_of(m), :]), split(s[z * layers + m]), TN)

    if not last:
        acc[...] = jnp.zeros_like(acc)

        @pl.loop(0, rows_n)
        def _(step):
            z = lax.rem(me + step, rows_n)
            each_block(z, lambda c: c.start())

            @pl.when(jnp.abs(z - me) < far)
            def _():
                each_share(z, lambda c: c.start())

        @pl.loop(0, rows_n)
        def _(step):
            z = lax.rem(me + step, rows_n)

            @pl.when(jnp.abs(z - me) < far)
            def _():
                add_product(z)

        return

    def each_out(z, m, act):
        for x in range(layers):
            @pl.when(jnp.bitwise_xor(m, layer) == x)
            def _():
                for h in range(per):
                    act(pltpu.make_async_copy(
                        o.at[z, m, :, pl.ds(h * size, size)],
                        outs[x * per + h].at[jnp.bitwise_xor(z, col)], out_sem.at[z, m, h]))

    far_z = far - me
    ends = jnp.abs(far_z - me) == far

    @pl.when(ends)
    def _():
        each_block(far_z, lambda c: c.start())
        each_share(far_z, lambda c: c.start())

    @pl.loop(0, rows_n)
    def _(z):
        @pl.when(jnp.abs(z - me) < far)
        def _():
            each_block(z, lambda c: c.start())

    acc[...] = refs[0][...]

    @pl.when(ends)
    def _():
        add_product(far_z)

    inner = split(acc[...])

    @pl.loop(0, rows_n)
    def _(z):
        @pl.when(jnp.abs(z - me) < far)
        def _():
            each_block(z, lambda c: c.wait())

        @pl.loop(0, layers)
        def _(m):
            o[z, m] = mm3(split(a[z, rows_of(m), :]), inner, NN)
            each_out(z, m, lambda c: c.start())

    @pl.loop(0, rows_n)
    def _(z):
        @pl.loop(0, layers)
        def _(m):
            each_out(z, m, lambda c: c.wait())


def gram_kernel(bundle, sizes, per, place_ref, *refs):
    cols_n, layers = sizes
    shares = cols_n * layers
    n_p = (bundle[-1] + 1) * per
    p_refs, outs, (left3, right3, g, sem) = refs[:n_p], refs[n_p:n_p + layers], refs[n_p + layers:]
    rows, size = p_refs[0].shape
    width = size * per
    col, layer = place_ref[1], place_ref[2]
    for t in range(bundle[-1] + 1):
        for h in range(per):
            hi, lo = split(p_refs[t * per + h][...])
            here = pl.ds(h * size, size)
            for n, part in enumerate((hi, hi, lo)):
                left3[t, n * rows:(n + 1) * rows, here] = part
            if t in bundle:
                for n, part in enumerate((hi, lo, hi)):
                    right3[bundle.index(t), n * rows:(n + 1) * rows, here] = part
    base, first = 0, 0
    copies = []
    for i, s in enumerate(bundle):
        for t in range(s, -1, -1):
            at = base + (s - t) * width
            g[at:at + width, :] = mm(left3[t], right3[i], TN)
        n = (s + 1) * width // shares
        for x in range(layers):
            for y in range(cols_n):
                share = jnp.bitwise_xor(layer, x) * cols_n + jnp.bitwise_xor(col, y)
                start = pl.multiple_of(base + share * n, 8)
                copies.append(pltpu.make_async_copy(
                    g.at[pl.ds(start, n), :], outs[x].at[y, pl.ds(first, n), :], sem.at[len(copies)]))
                copies[-1].start()
        base += (s + 1) * width
        first += n
    for c in copies:
        c.wait()


def gram_call(place, bundle, panels, sizes):
    cols_n, layers = sizes
    per = len(panels[0])
    rows, size = panels[0][0].shape
    width = size * per
    total = sum(s + 1 for s in bundle) * width
    flat = sum(panels[:bundle[-1] + 1], [])
    vmem = pl.BlockSpec(memory_space=pltpu.VMEM)
    return pl.pallas_call(
        functools.partial(gram_kernel, bundle, sizes, per),
        out_shape=[jax.ShapeDtypeStruct((cols_n, total // (cols_n * layers), width), F32)] * layers,
        in_specs=[pl.BlockSpec(memory_space=pltpu.SMEM)] + [vmem] * len(flat),
        out_specs=[pl.BlockSpec(memory_space=pl.ANY)] * layers,
        scratch_shapes=[
            pltpu.VMEM((bundle[-1] + 1, 3 * rows, width), BF16),
            pltpu.VMEM((len(bundle), 3 * rows, width), BF16),
            pltpu.VMEM((total, width), F32),
            pltpu.SemaphoreType.DMA((len(bundle) * cols_n * layers,)),
        ],
        compiler_params=pltpu.CompilerParams(vmem_limit_bytes=48 * 1024 * 1024),
        cost_estimate=pl.CostEstimate(flops=6 * total * width * rows, bytes_accessed=4 * total * width, transcendentals=0),
        name="gram",
    )(place, *flat)


def shift_by_xor(x, axis, step):
    n = lax.axis_size(axis)
    return lax.ppermute(x, axis, [(a, a ^ step) for a in range(n)])


def own_and_others(x, axis):
    return [x] + [shift_by_xor(x, axis, s) for s in range(1, lax.axis_size(axis))]


def chain(x, axis, direction):
    n = lax.axis_size(axis)
    pairs = [(a, a + direction) for a in range(n) if 0 <= a + direction < n]
    got = [x]
    for _ in range(n - 1):
        got.append(lax.ppermute(got[-1], axis, pairs))
    return got


def exchange_sum(parts, axis):
    came = [shift_by_xor(parts[s], axis, s) for s in range(1, len(parts))]
    return sum(came, parts[0])


def shards(wavefunction, start_block):
    sizes = rows_n, cols_n, layers = tuple(lax.axis_size(a) for a in ("row", "col", "layer"))
    row, col, layer = (lax.axis_index(a).astype(jnp.int32) for a in ("row", "col", "layer"))
    order_m = wavefunction.shape[0] * rows_n
    panel = start_block.shape[1]
    size = min(256, panel)
    per = panel // size
    place = jnp.stack([row, col, layer])

    width = wavefunction.shape[1] // layers
    own = lax.dynamic_slice_in_dim(wavefunction, layer * width, width, 1)
    chains = [(chain(cut, "row", 1), chain(cut, "row", -1)) for cut in jnp.split(own, 2)]
    blocks = [[c[0][0] for c in chains]]
    for s in range(1, rows_n):
        blocks += [[c[0][s] for c in chains], [c[1][s] for c in chains]]
    starts, s_places = [], []
    for s, part in enumerate(own_and_others(start_block, "col")):
        for t, piece in enumerate(own_and_others(part, "layer")):
            starts.append(piece)
            s_places.append((col ^ s) * layers + (layer ^ t))
    s_places = jnp.stack(s_places)
    inner = image_call(place, s_places, blocks[:-2], starts, sizes, per)
    images = image_call(place, s_places, blocks, starts, sizes, per, inner)
    panels = [[]]
    for h in range(per):
        image = exchange_sum([images[x * per + h] for x in range(layers)], "layer")
        panels[0].append(exchange_sum([image[s] for s in range(cols_n)], "col"))

    bundles = [[0, 1]] + [[s] for s in range(2, rows_n)]
    up = [(a, a + 1) for a in range(rows_n - 1)]
    g_arrays = []
    for s in range(rows_n):
        if s:
            panels.append([lax.ppermute(part, "row", up) for part in panels[-1]])
        for bundle in bundles:
            if bundle[-1] == s:
                gram = gram_call(place, bundle, panels, (cols_n, layers))
                gram = exchange_sum(gram, "layer")
                gram = [gram[y] for y in range(cols_n)]
                gram = exchange_sum(gram, "col")
                pieces = own_and_others(gram, "col")
                stack = jnp.stack(pieces)
                g_arrays.append(pieces + own_and_others(stack, "layer")[1:])
    places = jnp.stack([(layer ^ x) * cols_n + (col ^ s) for x in range(layers) for s in range(cols_n)])
    return factor_apply(place, places, bundles, g_arrays, cols_n, panels, size, math.sqrt(order_m))


def solution(mesh):
    placed = (P("row", "col"), P(("col", "layer"), "row"))

    return jax.shard_map(
        shards, mesh=mesh, in_specs=placed, out_specs=P(("col", "layer"), "row"), check_vma=False
    )
```

profile of v0, /device:TPU:29, one launch (start us, length us, event | category | flops | bytes accessed | tf_op | source)
XLA Modules:
  0.0 567.4 jit_solution(11918461708095266006)
XLA Ops:
  8.1 17.1 %collective-permute-done.17.refs_16_.refs_20_ = f32[512,512]{1,0:T(8,128)S(1)} collective-permute-done((f32[512,512]{1,0:T(8,128)}, f32[512,512]{1,0:T(8,128)S(1)}, u32[]{:S(2)}, u32[]{:S(2)}) %collective-permute-start.17) | collective-permute-done | bytes 1048608 | tf_op jit(solution)/shard_map/ppermute | solution.py:403
  26.5 22.3 %collective-permute-done.15.refs_14_.refs_18_ = f32[512,512]{1,0:T(8,128)} collective-permute-done((f32[512,512]{1,0:T(8,128)}, f32[512,512]{1,0:T(8,128)}, u32[]{:S(2)}, u32[]{:S(2)}) %collective-permute-start.15) | collective-permute-done | bytes 1048608 | tf_op jit(solution)/shard_map/ppermute | solution.py:403
  58.5 14.4 %collective-permute-done.2.refs_4_ = f32[512,512]{1,0:T(8,128)S(1)} collective-permute-done((f32[512,512]{1,0:T(8,128)S(1)}, f32[512,512]{1,0:T(8,128)S(1)}, u32[]{:S(2)}, u32[]{:S(2)}) %collective-permute-start.2) | collective-permute-done | bytes 1048608 | tf_op jit(solution)/shard_map/ppermute | solution.py:415
  83.8 11.5 %collective-permute-done.7.refs_9_ = f32[512,512]{1,0:T(8,128)} collective-permute-done((f32[512,512]{1,0:T(8,128)S(1)}, f32[512,512]{1,0:T(8,128)}, u32[]{:S(2)}, u32[]{:S(2)}) %collective-permute-start.7) | collective-permute-done | bytes 1048608 | tf_op jit(solution)/shard_map/ppermute | solution.py:415
  101.9 15.9 %collective-permute-done.6.refs_8_ = f32[512,512]{1,0:T(8,128)} collective-permute-done((f32[512,512]{1,0:T(8,128)S(1)}, f32[512,512]{1,0:T(8,128)}, u32[]{:S(2)}, u32[]{:S(2)}) %collective-permute-start.6) | collective-permute-done | bytes 1048608 | tf_op jit(solution)/shard_map/ppermute | solution.py:415
  125.8 10.6 %inner.1.refs_22_ = f32[512,512]{1,0:T(8,128)} custom-call(s32[3]{0:T(128)} %pad_add_fusion.place_ref.me_ref, s32[8]{0:T(128)} %stack.132.s_place_ref, f32[512,512]{1,0:T(8,128)} %copy-done.10, f32[512,512]{1,0:T(8,128)} %copy-done.9, f32[512,512]{1,0:T(8,128)} %copy-done.20, f32[512,512]{1,0:T(8,128)} %copy-done.18, f32[512,512]{1,0:T(8,128)} %copy-done.19, ...), custom_call_target="tpu_custom_call" | custom-call | flops 4831838208 | bytes 8388608 | tf_op jit(solution)/shard_map/inner/pallas_call | solution.py:214
  143.2 19.6 %collective-permute-done.10.refs_12_ = f32[512,512]{1,0:T(8,128)} collective-permute-done((f32[512,512]{1,0:T(8,128)}, f32[512,512]{1,0:T(8,128)}, u32[]{:S(2)}, u32[]{:S(2)}) %collective-permute-start.10) | collective-permute-done | bytes 1048608 | tf_op jit(solution)/shard_map/ppermute | solution.py:415
  165.7 15.0 %image.1 = (f32[4,512,256]{2,1,0:T(8,128)}, f32[4,512,256]{2,1,0:T(8,128)}, f32[4,512,256]{2,1,0:T(8,128)}, f32[4,512,256]{2,1,0:T(8,128)}) custom-call(s32[3]{0:T(128)} %pad_add_fusion.place_ref.me_ref, s32[8]{0:T(128)} %stack.132.s_place_ref, f32[512,512]{1,0:T(8,128)} %copy-done.10, f32[512,512]{1,0:T(8,128)} %copy-done.9, f32[512,512]{1,0:T(8,128)} %copy-done.20, ...), custom_call_target="tpu_custom_call" | custom-call | flops 8053063680 | bytes 8388608 | tf_op jit(solution)/shard_map/image/pallas_call | solution.py:214
  194.4 8.7 %collective-permute-done.20 = f32[512,256]{1,0:T(8,128)S(1)} collective-permute-done((f32[512,256]{1,0:T(8,128)S(1)}, f32[512,256]{1,0:T(8,128)S(1)}, u32[]{:S(2)}, u32[]{:S(2)}) %collective-permute-start.20) | collective-permute-done | bytes 524320 | tf_op jit(solution)/shard_map/ppermute | solution.py:403
  203.2 11.0 %collective-permute-done.22 = f32[512,256]{1,0:T(8,128)S(1)} collective-permute-done((f32[512,256]{1,0:T(8,128)S(1)}, f32[512,256]{1,0:T(8,128)S(1)}, u32[]{:S(2)}, u32[]{:S(2)}) %collective-permute-start.22) | collective-permute-done | bytes 524320 | tf_op jit(solution)/shard_map/ppermute | solution.py:403
  215.7 9.9 %collective-permute-done.24 = f32[512,256]{1,0:T(8,128)S(1)} collective-permute-done((f32[512,256]{1,0:T(8,128)S(1)}, f32[512,256]{1,0:T(8,128)S(1)}, u32[]{:S(2)}, u32[]{:S(2)}) %collective-permute-start.24) | collective-permute-done | bytes 524320 | tf_op jit(solution)/shard_map/ppermute | solution.py:403
  225.6 11.1 %collective-permute-done.26 = f32[512,256]{1,0:T(8,128)S(1)} collective-permute-done((f32[512,256]{1,0:T(8,128)S(1)}, f32[512,256]{1,0:T(8,128)S(1)}, u32[]{:S(2)}, u32[]{:S(2)}) %collective-permute-start.26) | collective-permute-done | bytes 524320 | tf_op jit(solution)/shard_map/ppermute | solution.py:403
  239.5 10.2 %collective-permute-done.28.refs_3_.refs_18_ = f32[512,256]{1,0:T(8,128)S(1)} collective-permute-done((f32[512,256]{1,0:T(8,128)S(1)}, f32[512,256]{1,0:T(8,128)S(1)}, u32[]{:S(2)}, u32[]{:S(2)}) %collective-permute-start.28) | collective-permute-done | bytes 524320 | tf_op jit(solution)/shard_map/ppermute | solution.py:457
  250.9 9.9 %collective-permute-done.37.refs_4_.refs_19_ = f32[512,256]{1,0:T(8,128)S(1)} collective-permute-done((f32[512,256]{1,0:T(8,128)S(1)}, f32[512,256]{1,0:T(8,128)S(1)}, u32[]{:S(2)}, u32[]{:S(2)}) %collective-permute-start.37) | collective-permute-done | bytes 524320 | tf_op jit(solution)/shard_map/ppermute | solution.py:457
  262.1 9.9 %collective-permute-done.38.refs_5_.refs_20_ = f32[512,256]{1,0:T(8,128)S(1)} collective-permute-done((f32[512,256]{1,0:T(8,128)S(1)}, f32[512,256]{1,0:T(8,128)S(1)}, u32[]{:S(2)}, u32[]{:S(2)}) %collective-permute-start.38) | collective-permute-done | bytes 524320 | tf_op jit(solution)/shard_map/ppermute | solution.py:457
  273.6 9.8 %collective-permute-done.47.refs_6_.refs_21_ = f32[512,256]{1,0:T(8,128)S(1)} collective-permute-done((f32[512,256]{1,0:T(8,128)S(1)}, f32[512,256]{1,0:T(8,128)S(1)}, u32[]{:S(2)}, u32[]{:S(2)}) %collective-permute-start.47) | collective-permute-done | bytes 524320 | tf_op jit(solution)/shard_map/ppermute | solution.py:457
  283.3 11.2 %collective-permute-done.48.refs_7_.refs_22_ = f32[512,256]{1,0:T(8,128)S(1)} collective-permute-done((f32[512,256]{1,0:T(8,128)S(1)}, f32[512,256]{1,0:T(8,128)S(1)}, u32[]{:S(2)}, u32[]{:S(2)}) %collective-permute-start.48) | collective-permute-done | bytes 524320 | tf_op jit(solution)/shard_map/ppermute | solution.py:457
  348.7 10.1 %collective-permute-done.52 = f32[256,512]{1,0:T(8,128)S(1)} collective-permute-done((f32[256,512]{1,0:T(8,128)S(1)}, f32[256,512]{1,0:T(8,128)S(1)}, u32[]{:S(2)}, u32[]{:S(2)}) %collective-permute-start.52) | collective-permute-done | bytes 524320 | tf_op jit(solution)/shard_map/ppermute | solution.py:403
  359.0 8.9 %collective-permute-done.51 = f32[256,512]{1,0:T(8,128)S(1)} collective-permute-done((f32[256,512]{1,0:T(8,128)S(1)}, f32[256,512]{1,0:T(8,128)S(1)}, u32[]{:S(2)}, u32[]{:S(2)}) %collective-permute-start.51) | collective-permute-done | bytes 524320 | tf_op jit(solution)/shard_map/ppermute | solution.py:403
  375.9 8.3 %collective-permute-done.42 = f32[192,512]{1,0:T(8,128)S(1)} collective-permute-done((f32[192,512]{1,0:T(8,128)S(1)}, f32[192,512]{1,0:T(8,128)S(1)}, u32[]{:S(2)}, u32[]{:S(2)}) %collective-permute-start.42) | collective-permute-done | bytes 393248 | tf_op jit(solution)/shard_map/ppermute | solution.py:403
  384.3 11.6 %collective-permute-done.41 = f32[192,512]{1,0:T(8,128)S(1)} collective-permute-done((f32[192,512]{1,0:T(8,128)S(1)}, f32[192,512]{1,0:T(8,128)S(1)}, u32[]{:S(2)}, u32[]{:S(2)}) %collective-permute-start.41) | collective-permute-done | bytes 393248 | tf_op jit(solution)/shard_map/ppermute | solution.py:403
  397.5 9.9 %collective-permute-done.54.refs_12_ = f32[256,512]{1,0:T(8,128)S(1)} collective-permute-done((f32[256,512]{1,0:T(8,128)S(1)}, f32[256,512]{1,0:T(8,128)S(1)}, u32[]{:S(2)}, u32[]{:S(2)}) %collective-permute-start.54) | collective-permute-done | bytes 524320 | tf_op jit(solution)/shard_map/ppermute | solution.py:403
  409.0 14.9 %collective-permute-done.34.refs_2_ = f32[192,512]{1,0:T(8,128)S(1)} collective-permute-done((f32[192,512]{1,0:T(8,128)S(1)}, f32[192,512]{1,0:T(8,128)S(1)}, u32[]{:S(2)}, u32[]{:S(2)}) %collective-permute-start.34) | collective-permute-done | bytes 393248 | tf_op jit(solution)/shard_map/ppermute | solution.py:403
  439.9 127.3 %factor.1 = f32[512,512]{1,0:T(8,128)} custom-call(s32[3]{0:T(128)} %pad_add_fusion.place_ref.me_ref, s32[8]{0:T(128)} %stack.123.order_ref, f32[192,512]{1,0:T(8,128)} %copy-done.14, f32[192,512]{1,0:T(8,128)} %copy-done.28, f32[192,512]{1,0:T(8,128)} %copy-done.27, f32[192,512]{1,0:T(8,128)} %copy-done.26, f32[4,192,512]{2,1,0:T(8,128)} %collective-permute-done.36.refs_4_, ...), custom_call_target="tpu_custom_call" | custom-call | flops 60000002048 | bytes 20000000 | tf_op jit(solution)/shard_map/factor/pallas_call | solution.py:167
  (182 shorter events, 157.5 us)
Async XLA Ops:
  1.2 47.6 %collective-permute-start.15 = (f32[512,512]{1,0:T(8,128)}, f32[512,512]{1,0:T(8,128)}, u32[]{:S(2)}, u32[]{:S(2)}) collective-permute-start(f32[512,512]{1,0:T(8,128)} %refs_14_.1), channel_id=1, source_target_pairs={{0,4},{2,6},{4,0},{6,2},{1,5},{3,7},{5,1},{7,3},{8,12},{10,14},{12... | collective-permute-start | bytes 3145736 | tf_op jit(solution)/shard_map/ppermute | solution.py:403
  2.4 48.5 %collective-permute-start.13 = (f32[512,512]{1,0:T(8,128)}, f32[512,512]{1,0:T(8,128)}, u32[]{:S(2)}, u32[]{:S(2)}) collective-permute-start(f32[512,512]{1,0:T(8,128)} %refs_14_.1), channel_id=1, source_target_pairs={{0,2},{2,0},{4,6},{6,4},{1,3},{3,1},{5,7},{7,5},{8,10},{10,8},{12,... | collective-permute-start | bytes 3145736 | tf_op jit(solution)/shard_map/ppermute | solution.py:403
  2.7 49.6 %collective-permute-start.12 = (f32[512,512]{1,0:T(8,128)}, f32[512,512]{1,0:T(8,128)}, u32[]{:S(2)}, u32[]{:S(2)}) collective-permute-start(f32[512,512]{1,0:T(8,128)} %refs_14_.1), channel_id=1, source_target_pairs={{0,1},{1,0},{2,3},{3,2},{4,5},{5,4},{6,7},{7,6},{8,9},{9,8},{10,11... | collective-permute-start | bytes 3145736 | tf_op jit(solution)/shard_map/ppermute | solution.py:403
  5.9 47.2 %collective-permute-start.3 = (f32[512,512]{1,0:T(8,128)S(1)}, f32[512,512]{1,0:T(8,128)S(1)}, u32[]{:S(2)}, u32[]{:S(2)}) collective-permute-start(f32[512,512]{1,0:T(8,128)S(1)} %get-tuple-element.25.refs_1_), channel_id=1, source_target_pairs={{8,0},{16,8},{24,16},{9,1},{17,9},{25,17},{10,2},{18,10},{26,18},{... | collective-permute-start | bytes 3145736 | tf_op jit(solution)/shard_map/ppermute | solution.py:415
  53.2 42.1 %collective-permute-start.7 = (f32[512,512]{1,0:T(8,128)S(1)}, f32[512,512]{1,0:T(8,128)}, u32[]{:S(2)}, u32[]{:S(2)}) collective-permute-start(f32[512,512]{1,0:T(8,128)S(1)} %collective-permute-done.3.refs_5_), channel_id=1, source_target_pairs={{8,0},{16,8},{24,16},{9,1},{17,9},{25,17},{10,2},{18,10},{26,18},{... | collective-permute-start | bytes 3145736 | tf_op jit(solution)/shard_map/ppermute | solution.py:415
  76.8 41.0 %collective-permute-start.6 = (f32[512,512]{1,0:T(8,128)S(1)}, f32[512,512]{1,0:T(8,128)}, u32[]{:S(2)}, u32[]{:S(2)}) collective-permute-start(f32[512,512]{1,0:T(8,128)S(1)} %collective-permute-done.2.refs_4_), channel_id=1, source_target_pairs={{8,0},{16,8},{24,16},{9,1},{17,9},{25,17},{10,2},{18,10},{26,18},{... | collective-permute-start | bytes 3145736 | tf_op jit(solution)/shard_map/ppermute | solution.py:415
  79.9 43.2 %collective-permute-start.4 = (f32[512,512]{1,0:T(8,128)S(1)}, f32[512,512]{1,0:T(8,128)}, u32[]{:S(2)}, u32[]{:S(2)}) collective-permute-start(f32[512,512]{1,0:T(8,128)S(1)} %collective-permute-done.refs_2_), channel_id=1, source_target_pairs={{0,8},{8,16},{16,24},{1,9},{9,17},{17,25},{2,10},{10,18},{18,26},{... | collective-permute-start | bytes 3145736 | tf_op jit(solution)/shard_map/ppermute | solution.py:415
  81.2 44.5 %collective-permute-start.14 = (f32[512,512]{1,0:T(8,128)}, f32[512,512]{1,0:T(8,128)}, u32[]{:S(2)}, u32[]{:S(2)}) collective-permute-start(f32[512,512]{1,0:T(8,128)} %collective-permute-done.13.refs_12_.refs_16_), channel_id=1, source_target_pairs={{0,1},{1,0},{2,3},{3,2},{4,5},{5,4},{6,7},{7,6},{8,9},{9,8},{10,11... | collective-permute-start | bytes 3145736 | tf_op jit(solution)/shard_map/ppermute | solution.py:403
  95.3 45.0 %collective-permute-start.11 = (f32[512,512]{1,0:T(8,128)}, f32[512,512]{1,0:T(8,128)}, u32[]{:S(2)}, u32[]{:S(2)}) collective-permute-start(f32[512,512]{1,0:T(8,128)} %collective-permute-done.7.refs_9_), channel_id=1, source_target_pairs={{8,0},{16,8},{24,16},{9,1},{17,9},{25,17},{10,2},{18,10},{26,18},{... | collective-permute-start | bytes 3145736 | tf_op jit(solution)/shard_map/ppermute | solution.py:415
  100.6 42.7 %collective-permute-start.9 = (f32[512,512]{1,0:T(8,128)}, f32[512,512]{1,0:T(8,128)}, u32[]{:S(2)}, u32[]{:S(2)}) collective-permute-start(f32[512,512]{1,0:T(8,128)} %collective-permute-done.5.refs_7_), channel_id=1, source_target_pairs={{0,8},{8,16},{16,24},{1,9},{9,17},{17,25},{2,10},{10,18},{18,26},{... | collective-permute-start | bytes 3145736 | tf_op jit(solution)/shard_map/ppermute | solution.py:415
  117.8 45.0 %collective-permute-start.10 = (f32[512,512]{1,0:T(8,128)}, f32[512,512]{1,0:T(8,128)}, u32[]{:S(2)}, u32[]{:S(2)}) collective-permute-start(f32[512,512]{1,0:T(8,128)} %collective-permute-done.6.refs_8_), channel_id=1, source_target_pairs={{8,0},{16,8},{24,16},{9,1},{17,9},{25,17},{10,2},{18,10},{26,18},{... | collective-permute-start | bytes 3145736 | tf_op jit(solution)/shard_map/ppermute | solution.py:415
  123.1 42.6 %collective-permute-start.8 = (f32[512,512]{1,0:T(8,128)}, f32[512,512]{1,0:T(8,128)}, u32[]{:S(2)}, u32[]{:S(2)}) collective-permute-start(f32[512,512]{1,0:T(8,128)} %collective-permute-done.4.refs_6_), channel_id=1, source_target_pairs={{0,8},{8,16},{16,24},{1,9},{9,17},{17,25},{2,10},{10,18},{18,26},{... | collective-permute-start | bytes 3145736 | tf_op jit(solution)/shard_map/ppermute | solution.py:415
  193.0 32.6 %collective-permute-start.24 = (f32[512,256]{1,0:T(8,128)S(1)}, f32[512,256]{1,0:T(8,128)S(1)}, u32[]{:S(2)}, u32[]{:S(2)}) collective-permute-start(f32[512,256]{1,0:T(8,128)S(1)} %get-tuple-element.30), channel_id=1, source_target_pairs={{0,2},{2,0},{4,6},{6,4},{1,3},{3,1},{5,7},{7,5},{8,10},{10,8},{12,... | collective-permute-start | bytes 1572872 | tf_op jit(solution)/shard_map/ppermute | solution.py:403
  193.1 43.6 %collective-permute-start.26 = (f32[512,256]{1,0:T(8,128)S(1)}, f32[512,256]{1,0:T(8,128)S(1)}, u32[]{:S(2)}, u32[]{:S(2)}) collective-permute-start(f32[512,256]{1,0:T(8,128)S(1)} %get-tuple-element.31), channel_id=1, source_target_pairs={{0,6},{2,4},{4,2},{6,0},{1,7},{3,5},{5,3},{7,1},{8,14},{10,12},{12... | collective-permute-start | bytes 1572872 | tf_op jit(solution)/shard_map/ppermute | solution.py:403
  203.0 33.6 %collective-permute-start.25 = (f32[512,256]{1,0:T(8,128)S(1)}, f32[512,256]{1,0:T(8,128)S(1)}, u32[]{:S(2)}, u32[]{:S(2)}) collective-permute-start(f32[512,256]{1,0:T(8,128)S(1)} %get-tuple-element.32), channel_id=1, source_target_pairs={{0,4},{2,6},{4,0},{6,2},{1,5},{3,7},{5,1},{7,3},{8,12},{10,14},{12... | collective-permute-start | bytes 1572872 | tf_op jit(solution)/shard_map/ppermute | solution.py:403
  337.2 32.1 %collective-permute-start.35 = (f32[192,512]{1,0:T(8,128)S(1)}, f32[192,512]{1,0:T(8,128)S(1)}, u32[]{:S(2)}, u32[]{:S(2)}) collective-permute-start(f32[192,512]{1,0:T(8,128)S(1)} %fusion.14.refs_0_), channel_id=1, source_target_pairs={{0,6},{2,4},{4,2},{6,0},{1,7},{3,5},{5,3},{7,1},{8,14},{10,12},{12... | collective-permute-start | bytes 1179656 | tf_op jit(solution)/shard_map/ppermute | solution.py:403
  339.4 35.3 %collective-permute-start.40 = (f32[192,512]{1,0:T(8,128)S(1)}, f32[192,512]{1,0:T(8,128)S(1)}, u32[]{:S(2)}, u32[]{:S(2)}) collective-permute-start(f32[192,512]{1,0:T(8,128)S(1)} %get-tuple-element.36), channel_id=1, source_target_pairs={{0,2},{2,0},{4,6},{6,4},{1,3},{3,1},{5,7},{7,5},{8,10},{10,8},{12,... | collective-permute-start | bytes 1179656 | tf_op jit(solution)/shard_map/ppermute | solution.py:403
  346.5 37.7 %collective-permute-start.42 = (f32[192,512]{1,0:T(8,128)S(1)}, f32[192,512]{1,0:T(8,128)S(1)}, u32[]{:S(2)}, u32[]{:S(2)}) collective-permute-start(f32[192,512]{1,0:T(8,128)S(1)} %get-tuple-element.37), channel_id=1, source_target_pairs={{0,6},{2,4},{4,2},{6,0},{1,7},{3,5},{5,3},{7,1},{8,14},{10,12},{12... | collective-permute-start | bytes 1179656 | tf_op jit(solution)/shard_map/ppermute | solution.py:403
  358.8 37.1 %collective-permute-start.41 = (f32[192,512]{1,0:T(8,128)S(1)}, f32[192,512]{1,0:T(8,128)S(1)}, u32[]{:S(2)}, u32[]{:S(2)}) collective-permute-start(f32[192,512]{1,0:T(8,128)S(1)} %get-tuple-element.38), channel_id=1, source_target_pairs={{0,4},{2,6},{4,0},{6,2},{1,5},{3,7},{5,1},{7,3},{8,12},{10,14},{12... | collective-permute-start | bytes 1179656 | tf_op jit(solution)/shard_map/ppermute | solution.py:403
  369.3 38.1 %collective-permute-start.54 = (f32[256,512]{1,0:T(8,128)S(1)}, f32[256,512]{1,0:T(8,128)S(1)}, u32[]{:S(2)}, u32[]{:S(2)}) collective-permute-start(f32[256,512]{1,0:T(8,128)S(1)} %fusion.2.refs_10_), channel_id=1, source_target_pairs={{0,4},{2,6},{4,0},{6,2},{1,5},{3,7},{5,1},{7,3},{8,12},{10,14},{12... | collective-permute-start | bytes 1572872 | tf_op jit(solution)/shard_map/ppermute | solution.py:403
  374.7 32.9 %collective-permute-start.53 = (f32[256,512]{1,0:T(8,128)S(1)}, f32[256,512]{1,0:T(8,128)S(1)}, u32[]{:S(2)}, u32[]{:S(2)}) collective-permute-start(f32[256,512]{1,0:T(8,128)S(1)} %fusion.2.refs_10_), channel_id=1, source_target_pairs={{0,2},{2,0},{4,6},{6,4},{1,3},{3,1},{5,7},{7,5},{8,10},{10,8},{12,... | collective-permute-start | bytes 1572872 | tf_op jit(solution)/shard_map/ppermute | solution.py:403
  384.2 39.8 %collective-permute-start.34 = (f32[192,512]{1,0:T(8,128)S(1)}, f32[192,512]{1,0:T(8,128)S(1)}, u32[]{:S(2)}, u32[]{:S(2)}) collective-permute-start(f32[192,512]{1,0:T(8,128)S(1)} %fusion.14.refs_0_), channel_id=1, source_target_pairs={{0,4},{2,6},{4,0},{6,2},{1,5},{3,7},{5,1},{7,3},{8,12},{10,14},{12... | collective-permute-start | bytes 1179656 | tf_op jit(solution)/shard_map/ppermute | solution.py:403
  395.9 32.5 %collective-permute-start.33 = (f32[192,512]{1,0:T(8,128)S(1)}, f32[192,512]{1,0:T(8,128)S(1)}, u32[]{:S(2)}, u32[]{:S(2)}) collective-permute-start(f32[192,512]{1,0:T(8,128)S(1)} %fusion.14.refs_0_), channel_id=1, source_target_pairs={{0,2},{2,0},{4,6},{6,4},{1,3},{3,1},{5,7},{7,5},{8,10},{10,8},{12,... | collective-permute-start | bytes 1179656 | tf_op jit(solution)/shard_map/ppermute | solution.py:403
  397.3 32.5 %collective-permute-start.45 = (f32[192,512]{1,0:T(8,128)S(1)}, f32[192,512]{1,0:T(8,128)S(1)}, u32[]{:S(2)}, u32[]{:S(2)}) collective-permute-start(f32[192,512]{1,0:T(8,128)S(1)} %fusion.11.refs_5_), channel_id=1, source_target_pairs={{0,6},{2,4},{4,2},{6,0},{1,7},{3,5},{5,3},{7,1},{8,14},{10,12},{12... | collective-permute-start | bytes 1179656 | tf_op jit(solution)/shard_map/ppermute | solution.py:403
  (65 other events, 2000.1 us)
where the time goes:
time: 568 us; the launch traced here: 567 us
  waiting for transfers between devices  303 us (53%)
  Pallas kernels  170 us (30%)
  starting transfers between devices  82.3 us (14%)
  other arithmetic  7.86 us (1%)
    ppermute x39, waiting for transfers between devices, shift_by_xor(): return lax.ppermute(x, axis, [(a, a ^ step) for a in range(n)])  178 us
    pallas_call x1, Pallas kernels, factor_apply(): pl.pallas_call(functools.partial(factor_kernel, blocks, size, groups, bun...  127 us
    ppermute x12, waiting for transfers between devices, chain(): got.append(lax.ppermute(got[-1], axis, pairs))  73.7 us
    ppermute x6, waiting for transfers between devices, shards(): panels.append([lax.ppermute(part, 'row', up) for part in panels[-1]])  51 us
    ppermute x39, starting transfers between devices, shift_by_xor(): return lax.ppermute(x, axis, [(a, a ^ step) for a in range(n)])  43.5 us
    ppermute x12, starting transfers between devices, chain(): got.append(lax.ppermute(got[-1], axis, pairs))  30.9 us
    pallas_call x2, Pallas kernels, image_call(): pl.pallas_call(functools.partial(image_kernel, sizes, cuts, per, last), o...  25.6 us
    pallas_call x3, Pallas kernels, gram_call(): pl.pallas_call(functools.partial(gram_kernel, bundle, sizes, per), out_sh...  16.8 us
  transfers between devices with their start and end apart: 57, of which 33 were waited for; matrix products, arithmetic and copies ran while one was open for 2% of the time, Pallas kernels for 4%

commit v1 on v0

--- a/solution.py
+++ b/solution.py
@@ -10,6 +10,7 @@
 NT = (((1,), (1,)), ((), ()))
 TN = (((0,), (0,)), ((), ()))
 STEPS = 5
+BESIDE = 2
 
 
 def mm(a, b, dims):
@@ -33,7 +34,7 @@
     return jnp.where(rows > cols, x, jnp.where(rows == cols, 0.5 * x, 0.0))
 
 
-def inverse_factor(block, out_ref, work_ref):
+def inverse_factor(block, out_ref, work_ref, beside):
     n = block.shape[0]
     rows, cols = iotas(n)
     eye = (rows == cols).astype(F32)
@@ -42,19 +43,23 @@
     scale_col = lax.rsqrt(jnp.sum(on_diag, axis=1, keepdims=True))
     scaled = block * scale_row * scale_col
     w = scaled
-    half = lower_half(w - eye, rows, cols)
-    x = eye - half
-    hb = half.astype(BF16)
-    w = w - mm(hb, w.astype(BF16), NN)
-    w = w - mm(w.astype(BF16), hb, NT)
-    for _ in range(STEPS - 1):
-        hb = lower_half(w - eye, rows, cols).astype(BF16)
-        x = x - mm(hb, x.astype(BF16), NN)
-        w = w - mm(hb, w.astype(BF16), NN)
+    x = eye
+    for step in range(STEPS):
+        half = lower_half(w - eye, rows, cols)
+        hb = half.astype(BF16)
+        moved = mm(hb, w.astype(BF16), NN)
+        x = x - (mm(hb, x.astype(BF16), NN) if step else half)
+        beside()
+        w = w - moved
         w = w - mm(w.astype(BF16), hb, NT)
+        beside()
     xs = split(x)
-    error = mm3(split(mm3(xs, split(scaled), NN)), xs, NT) - eye
+    product = mm3(xs, split(scaled), NN)
+    beside()
+    error = mm3(split(product), xs, NT) - eye
+    beside()
     x = x - mm3(split(lower_half(error, rows, cols)), xs, NN)
+    beside()
     out_ref[...] = x * scale_row
     size = jnp.sum(error * error)
 
@@ -78,14 +83,27 @@
         out_ref[...] = out_ref[...] * lax.rsqrt(pivots)
 
 
-def factor_kernel(blocks, size, groups, bundles, shares, swaps, scale, me_ref, order_ref, *refs):
+def task_table(blocks, per, extra):
+    lists = []
+    for count in range(per, blocks + 1, per):
+        mine = []
+        for j in range(count - 1, 0, -1):
+            mine += [(i, j) for i in list(range(j + 1, count)) + list(range(blocks, blocks + extra))] + [(j, j)]
+        lists.append(mine)
+    most = max(len(mine) for mine in lists) + 1
+    idle = (blocks + extra, blocks - 1)
+    return most, jnp.array([mine + [idle] * (most - len(mine)) for mine in lists], jnp.int32).reshape(-1)
+
+
+def factor_kernel(blocks, size, groups, bundles, shares, swaps, scale, extra, most, me_ref, order_ref, table_ref, *refs):
     per = blocks // groups
     width = per * size
     arrays = shares + swaps
     g_refs = [refs[n * arrays:(n + 1) * arrays] for n in range(len(bundles))]
     refs = refs[len(bundles) * arrays:]
     b_refs = [refs[s * per:(s + 1) * per] for s in range(groups)]
-    out_ref, g, b, left3, right3, x_ref, work_ref, sem = refs[groups * per:]
+    out_ref, g, left3, right3, x_ref, work_ref, sem = refs[groups * per:]
+    tall = b_refs[0][0].shape[0]
     me = me_ref[0]
     pieces = shares * (1 + swaps)
     copies = [[] for _ in range(groups)]
@@ -105,7 +123,8 @@
                 first += rows
     for s in range(groups):
         for h in range(per):
-            copies[s].append(pltpu.make_async_copy(b_refs[s][h], b.at[(me - s) * per + h], sem.at[n_sem]))
+            copies[s].append(pltpu.make_async_copy(
+                b_refs[s][h], g.at[(me - s) * per + h, pl.ds(blocks * size, tall), :], sem.at[n_sem]))
             n_sem += 1
 
     def each_group(wanted, act):
@@ -120,40 +139,57 @@
     each_group(lambda s: s == me, lambda c: c.wait())
     count = (me + 1) * per
 
-    def rows_of(i):
-        return pl.ds(pl.multiple_of(i * size, size), size)
+    def rows_of(i, n=1):
+        return pl.ds(pl.multiple_of(i * size, size), n * size)
+
+    def update(t, limit):
+        at = 2 * (me * most + jnp.where(t < limit, t, most - 1))
+        i, j = table_ref[at], table_ref[at + 1]
+        g[j, rows_of(i), :] = g[j, rows_of(i), :] - mm(left3[i], right3[j], NT)
 
     @pl.loop(0, count)
     def _(k):
-        inverse_factor(g[k, rows_of(k), :], x_ref, work_ref)
-        xs = split(x_ref[...])
-
-        @pl.when(k == 0)
+        @pl.when(k == 1)
         def _():
             each_group(lambda s: s < me, lambda c: c.wait())
 
-        done = mm3(split(b[k]), xs, NT)
-        high, low = split(done)
-        done3 = jnp.concatenate([high, high, low], axis=1)
-
-        @pl.when(k >= me * per)
+        @pl.when(k > 0)
         def _():
-            out_ref[:, pl.ds(pl.multiple_of((k - me * per) * size, size), size)] = done * scale
-
-        @pl.loop(k + 1, count)
-        def _(i):
-            hi, lo = split(mm3(split(g[k, rows_of(i), :]), xs, NT))
-            left3[i] = jnp.concatenate([hi, hi, lo], axis=1)
-            right3[i] = jnp.concatenate([hi, lo, hi], axis=1)
-
-        @pl.loop(k + 1, count)
-        def _(j):
-            right = right3[j]
-            b[j] = b[j] - mm(done3, right, NT)
-
-            @pl.loop(j, count)
-            def _(i):
-                g[j, rows_of(i), :] = g[j, rows_of(i), :] - mm(left3[i], right, NT)
+            g[k, rows_of(k), :] = g[k, rows_of(k), :] - mm(left3[k], right3[k], NT)
+
+        left = count - k
+        tasks = jnp.where(k > 0, left * (left + 1) // 2 + left * extra - 1, 0)
+        issued = []
+
+        def beside():
+            for _ in range(BESIDE):
+                update(len(issued), tasks)
+                issued.append(None)
+
+        inverse_factor(g[k, rows_of(k), :], x_ref, work_ref, beside)
+
+        @pl.loop(len(issued), jnp.maximum(tasks, len(issued)))
+        def _(t):
+            update(t, tasks)
+
+        hi, lo = split(x_ref[...])
+        x3 = jnp.concatenate([hi, lo, hi], axis=1)
+
+        @pl.loop(0, (blocks + extra - k) // 2)
+        def _(c):
+            i = k + 1 + 2 * c
+            hi, lo = split(g[k, rows_of(i, 2), :])
+            done = mm(jnp.concatenate([hi, hi, lo], axis=1), x3, NT)
+            g[k, rows_of(i, 2), :] = done
+            hi, lo = split(done)
+            for n in range(2):
+                part = slice(n * size, (n + 1) * size)
+                left3[i + n] = jnp.concatenate([hi[part], hi[part], lo[part]], axis=1)
+                right3[i + n] = jnp.concatenate([hi[part], lo[part], hi[part]], axis=1)
+
+    rows = out_ref.shape[0]
+    for h in range(per):
+        out_ref[:, h * size:(h + 1) * size] = g[me * per + h, blocks * size:blocks * size + rows, :] * scale
 
 
 def factor_apply(me, order, bundles, g_arrays, shares, b_groups, size, scale):
@@ -161,19 +197,20 @@
     swaps = len(g_arrays[0]) - shares
     rows = b_groups[0][0].shape[0]
     blocks = groups * per
+    extra = -(-rows // size)
+    most, table = task_table(blocks, per, extra)
     any_spec = pl.BlockSpec(memory_space=pl.ANY)
     smem = pl.BlockSpec(memory_space=pltpu.SMEM)
     arrays = sum(g_arrays, []) + sum(b_groups, [])
     return pl.pallas_call(
-        functools.partial(factor_kernel, blocks, size, groups, bundles, shares, swaps, scale),
+        functools.partial(factor_kernel, blocks, size, groups, bundles, shares, swaps, scale, extra, most),
         out_shape=jax.ShapeDtypeStruct((rows, per * size), F32),
-        in_specs=[smem, smem] + [any_spec] * len(arrays),
+        in_specs=[smem, smem, smem] + [any_spec] * len(arrays),
         out_specs=pl.BlockSpec(memory_space=pltpu.VMEM),
         scratch_shapes=[
-            pltpu.VMEM((blocks, blocks * size, size), F32),
-            pltpu.VMEM((blocks, rows, size), F32),
-            pltpu.VMEM((blocks, size, 3 * size), BF16),
-            pltpu.VMEM((blocks, size, 3 * size), BF16),
+            pltpu.VMEM((blocks, (blocks + extra + 1) * size, size), F32),
+            pltpu.VMEM((blocks + extra + 1, size, 3 * size), BF16),
+            pltpu.VMEM((blocks + extra + 1, size, 3 * size), BF16),
             pltpu.VMEM((size, size), F32),
             pltpu.VMEM((size, size), F32),
             pltpu.SemaphoreType.DMA((groups * per * (shares * (1 + swaps) + 1),)),
@@ -181,7 +218,7 @@
         compiler_params=pltpu.CompilerParams(vmem_limit_bytes=56 * 1024 * 1024),
         cost_estimate=pl.CostEstimate(flops=6 * 10**10, bytes_accessed=2 * 10**7, transcendentals=0),
         name="factor",
-    )(me, order, *arrays)
+    )(me, order, table, *arrays)
 
 
 def image_call(places, s_places, blocks, starts, sizes, per, inner=None):
@@ -403,8 +440,24 @@
     return lax.ppermute(x, axis, [(a, a ^ step) for a in range(n)])
 
 
-def own_and_others(x, axis):
+def own_and_others(x, axis, heavy=0):
+    if heavy and lax.axis_size(axis) == 4:
+        near, side = shift_by_xor(x, axis, 3 ^ heavy), shift_by_xor(x, axis, heavy)
+        got = {0: x, 3 ^ heavy: near, heavy: side, 3: shift_by_xor(near, axis, heavy)}
+        return [got[s] for s in range(4)]
     return [x] + [shift_by_xor(x, axis, s) for s in range(1, lax.axis_size(axis))]
+
+
+def exchange_sum(parts, axis, heavy=0):
+    if heavy and len(parts) == 4:
+        light = 3 ^ heavy
+        through = shift_by_xor(parts[3], axis, heavy)
+        came = shift_by_xor(parts[heavy], axis, heavy)
+        onward = parts[light] + through
+        onward = shift_by_xor(onward, axis, light)
+        return parts[0] + came + onward
+    came = [shift_by_xor(parts[s], axis, s) for s in range(1, len(parts))]
+    return sum(came, parts[0])
 
 
 def chain(x, axis, direction):
@@ -414,11 +467,6 @@
     for _ in range(n - 1):
         got.append(lax.ppermute(got[-1], axis, pairs))
     return got
-
-
-def exchange_sum(parts, axis):
-    came = [shift_by_xor(parts[s], axis, s) for s in range(1, len(parts))]
-    return sum(came, parts[0])
 
 
 def shards(wavefunction, start_block):
@@ -447,7 +495,7 @@
     panels = [[]]
     for h in range(per):
         image = exchange_sum([images[x * per + h] for x in range(layers)], "layer")
-        panels[0].append(exchange_sum([image[s] for s in range(cols_n)], "col"))
+        panels[0].append(exchange_sum([image[s] for s in range(cols_n)], "col", 1 + h % 2))
 
     bundles = [[0, 1]] + [[s] for s in range(2, rows_n)]
     up = [(a, a + 1) for a in range(rows_n - 1)]
@@ -460,10 +508,9 @@
                 gram = gram_call(place, bundle, panels, (cols_n, layers))
                 gram = exchange_sum(gram, "layer")
                 gram = [gram[y] for y in range(cols_n)]
-                gram = exchange_sum(gram, "col")
-                pieces = own_and_others(gram, "col")
-                stack = jnp.stack(pieces)
-                g_arrays.append(pieces + own_and_others(stack, "layer")[1:])
+                gram = exchange_sum(gram, "col", 1)
+                pieces = own_and_others(gram, "col", 2)
+                g_arrays.append(pieces + own_and_others(jnp.stack(pieces), "layer")[1:])
     places = jnp.stack([(layer ^ x) * cols_n + (col ^ s) for x in range(layers) for s in range(cols_n)])
     return factor_apply(place, places, bundles, g_arrays, cols_n, panels, size, math.sqrt(order_m))
 
@@ -471,6 +518,4 @@
 def solution(mesh):
     placed = (P("row", "col"), P(("col", "layer"), "row"))
 
-    return jax.shard_map(
-        shards, mesh=mesh, in_specs=placed, out_specs=P(("col", "layer"), "row"), check_vma=False
-    )
+    return jax.shard_map(shards, mesh=mesh, in_specs=placed, out_specs=P(("col", "layer"), "row"), check_vma=False)

time: 568 us -> 537 us (0.945)
  Pallas kernels: 170 us -> 150 us
  starting transfers between devices: 82.3 us -> 76 us
  waiting for transfers between devices: 303 us -> 297 us
    pallas_call x1, Pallas kernels: 127 us -> 108 us  [factor_apply(): pl.pallas_call(functools.partial(factor_kernel, blocks, size, groups, bun...]
    ppermute x39, waiting for transfers between devices: 178 us -> 172 us  [shift_by_xor(): return lax.ppermute(x, axis, [(a, a ^ step) for a in range(n)])]
    ppermute x39, starting transfers between devices: 43.5 us -> 37.2 us  [shift_by_xor(): return lax.ppermute(x, axis, [(a, a ^ step) for a in range(n)])]
  transfers between devices with their start and end apart: 57 -> 57, of which waited for: 33 -> 34; matrix products, arithmetic and copies ran while one was open for 2% -> 2% of each run, Pallas kernels for 4% -> 4%
where the time goes in v1:
time: 537 us; the launch traced here: 536 us
  waiting for transfers between devices  297 us (55%)
  Pallas kernels  150 us (28%)
  starting transfers between devices  76 us (14%)
  other arithmetic  7.87 us (1%)
    ppermute x39, waiting for transfers between devices, shift_by_xor(): return lax.ppermute(x, axis, [(a, a ^ step) for a in range(n)])  172 us
    pallas_call x1, Pallas kernels, factor_apply(): pl.pallas_call(functools.partial(factor_kernel, blocks, size, groups, bun...  108 us
    ppermute x12, waiting for transfers between devices, chain(): got.append(lax.ppermute(got[-1], axis, pairs))  73.7 us
    ppermute x6, waiting for transfers between devices, shards(): panels.append([lax.ppermute(part, 'row', up) for part in panels[-1]])  51.2 us
    ppermute x39, starting transfers between devices, shift_by_xor(): return lax.ppermute(x, axis, [(a, a ^ step) for a in range(n)])  37.2 us
    ppermute x12, starting transfers between devices, chain(): got.append(lax.ppermute(got[-1], axis, pairs))  30.9 us
    pallas_call x2, Pallas kernels, image_call(): pl.pallas_call(functools.partial(image_kernel, sizes, cuts, per, last), o...  25.6 us
    pallas_call x3, Pallas kernels, gram_call(): pl.pallas_call(functools.partial(gram_kernel, bundle, sizes, per), out_sh...  16.9 us
  transfers between devices with their start and end apart: 57, of which 34 were waited for; matrix products, arithmetic and copies ran while one was open for 2% of the time, Pallas kernels for 4%

profile of v1, /device:TPU:29, one launch (start us, length us, event | category | flops | bytes accessed | tf_op | source)
XLA Modules:
  0.0 536.2 jit_solution(7227386449677609437)
XLA Ops:
  8.1 17.1 %collective-permute-done.17.refs_16_.refs_20_ = f32[512,512]{1,0:T(8,128)S(1)} collective-permute-done((f32[512,512]{1,0:T(8,128)}, f32[512,512]{1,0:T(8,128)S(1)}, u32[]{:S(2)}, u32[]{:S(2)}) %collective-permute-start.17) | collective-permute-done | bytes 1048608 | tf_op jit(solution)/shard_map/ppermute | solution.py:440
  26.5 22.3 %collective-permute-done.15.refs_14_.refs_18_ = f32[512,512]{1,0:T(8,128)} collective-permute-done((f32[512,512]{1,0:T(8,128)}, f32[512,512]{1,0:T(8,128)}, u32[]{:S(2)}, u32[]{:S(2)}) %collective-permute-start.15) | collective-permute-done | bytes 1048608 | tf_op jit(solution)/shard_map/ppermute | solution.py:440
  58.5 14.4 %collective-permute-done.2.refs_4_ = f32[512,512]{1,0:T(8,128)S(1)} collective-permute-done((f32[512,512]{1,0:T(8,128)S(1)}, f32[512,512]{1,0:T(8,128)S(1)}, u32[]{:S(2)}, u32[]{:S(2)}) %collective-permute-start.2) | collective-permute-done | bytes 1048608 | tf_op jit(solution)/shard_map/ppermute | solution.py:468
  83.8 11.5 %collective-permute-done.7.refs_9_ = f32[512,512]{1,0:T(8,128)} collective-permute-done((f32[512,512]{1,0:T(8,128)S(1)}, f32[512,512]{1,0:T(8,128)}, u32[]{:S(2)}, u32[]{:S(2)}) %collective-permute-start.7) | collective-permute-done | bytes 1048608 | tf_op jit(solution)/shard_map/ppermute | solution.py:468
  101.9 15.9 %collective-permute-done.6.refs_8_ = f32[512,512]{1,0:T(8,128)} collective-permute-done((f32[512,512]{1,0:T(8,128)S(1)}, f32[512,512]{1,0:T(8,128)}, u32[]{:S(2)}, u32[]{:S(2)}) %collective-permute-start.6) | collective-permute-done | bytes 1048608 | tf_op jit(solution)/shard_map/ppermute | solution.py:468
  125.8 10.6 %inner.1.refs_22_ = f32[512,512]{1,0:T(8,128)} custom-call(s32[3]{0:T(128)} %pad_add_fusion.place_ref.me_ref, s32[8]{0:T(128)} %stack.132.s_place_ref, f32[512,512]{1,0:T(8,128)} %copy-done.10, f32[512,512]{1,0:T(8,128)} %copy-done.9, f32[512,512]{1,0:T(8,128)} %copy-done.20, f32[512,512]{1,0:T(8,128)} %copy-done.18, f32[512,512]{1,0:T(8,128)} %copy-done.19, ...), custom_call_target="tpu_custom_call" | custom-call | flops 4831838208 | bytes 8388608 | tf_op jit(solution)/shard_map/inner/pallas_call | solution.py:251
  143.2 19.6 %collective-permute-done.10.refs_12_ = f32[512,512]{1,0:T(8,128)} collective-permute-done((f32[512,512]{1,0:T(8,128)}, f32[512,512]{1,0:T(8,128)}, u32[]{:S(2)}, u32[]{:S(2)}) %collective-permute-start.10) | collective-permute-done | bytes 1048608 | tf_op jit(solution)/shard_map/ppermute | solution.py:468
  165.7 15.0 %image.1 = (f32[4,512,256]{2,1,0:T(8,128)}, f32[4,512,256]{2,1,0:T(8,128)}, f32[4,512,256]{2,1,0:T(8,128)}, f32[4,512,256]{2,1,0:T(8,128)}) custom-call(s32[3]{0:T(128)} %pad_add_fusion.place_ref.me_ref, s32[8]{0:T(128)} %stack.132.s_place_ref, f32[512,512]{1,0:T(8,128)} %copy-done.10, f32[512,512]{1,0:T(8,128)} %copy-done.9, f32[512,512]{1,0:T(8,128)} %copy-done.20, ...), custom_call_target="tpu_custom_call" | custom-call | flops 8053063680 | bytes 8388608 | tf_op jit(solution)/shard_map/image/pallas_call | solution.py:251
  193.2 9.8 %collective-permute-done.21 = f32[512,256]{1,0:T(8,128)S(1)} collective-permute-done((f32[512,256]{1,0:T(8,128)S(1)}, f32[512,256]{1,0:T(8,128)S(1)}, u32[]{:S(2)}, u32[]{:S(2)}) %collective-permute-start.21) | collective-permute-done | bytes 524320 | tf_op jit(solution)/shard_map/ppermute | solution.py:440
  205.1 9.2 %collective-permute-done.20 = f32[512,256]{1,0:T(8,128)S(1)} collective-permute-done((f32[512,256]{1,0:T(8,128)S(1)}, f32[512,256]{1,0:T(8,128)S(1)}, u32[]{:S(2)}, u32[]{:S(2)}) %collective-permute-start.20) | collective-permute-done | bytes 524320 | tf_op jit(solution)/shard_map/ppermute | solution.py:440
  216.0 9.8 %collective-permute-done.24 = f32[512,256]{1,0:T(8,128)S(1)} collective-permute-done((f32[512,256]{1,0:T(8,128)S(1)}, f32[512,256]{1,0:T(8,128)S(1)}, u32[]{:S(2)}, u32[]{:S(2)}) %collective-permute-start.24) | collective-permute-done | bytes 524320 | tf_op jit(solution)/shard_map/ppermute | solution.py:440
  228.6 10.4 %collective-permute-done.28.refs_3_.refs_18_ = f32[512,256]{1,0:T(8,128)S(1)} collective-permute-done((f32[512,256]{1,0:T(8,128)S(1)}, f32[512,256]{1,0:T(8,128)S(1)}, u32[]{:S(2)}, u32[]{:S(2)}) %collective-permute-start.28) | collective-permute-done | bytes 524320 | tf_op jit(solution)/shard_map/ppermute | solution.py:505
  240.2 9.9 %collective-permute-done.37.refs_4_.refs_19_ = f32[512,256]{1,0:T(8,128)S(1)} collective-permute-done((f32[512,256]{1,0:T(8,128)S(1)}, f32[512,256]{1,0:T(8,128)S(1)}, u32[]{:S(2)}, u32[]{:S(2)}) %collective-permute-start.37) | collective-permute-done | bytes 524320 | tf_op jit(solution)/shard_map/ppermute | solution.py:505
  251.4 9.9 %collective-permute-done.38.refs_5_.refs_20_ = f32[512,256]{1,0:T(8,128)S(1)} collective-permute-done((f32[512,256]{1,0:T(8,128)S(1)}, f32[512,256]{1,0:T(8,128)S(1)}, u32[]{:S(2)}, u32[]{:S(2)}) %collective-permute-start.38) | collective-permute-done | bytes 524320 | tf_op jit(solution)/shard_map/ppermute | solution.py:505
  262.9 9.8 %collective-permute-done.47.refs_6_.refs_21_ = f32[512,256]{1,0:T(8,128)S(1)} collective-permute-done((f32[512,256]{1,0:T(8,128)S(1)}, f32[512,256]{1,0:T(8,128)S(1)}, u32[]{:S(2)}, u32[]{:S(2)}) %collective-permute-start.47) | collective-permute-done | bytes 524320 | tf_op jit(solution)/shard_map/ppermute | solution.py:505
  272.6 11.2 %collective-permute-done.48.refs_7_.refs_22_ = f32[512,256]{1,0:T(8,128)S(1)} collective-permute-done((f32[512,256]{1,0:T(8,128)S(1)}, f32[512,256]{1,0:T(8,128)S(1)}, u32[]{:S(2)}, u32[]{:S(2)}) %collective-permute-start.48) | collective-permute-done | bytes 524320 | tf_op jit(solution)/shard_map/ppermute | solution.py:505
  308.2 10.9 %collective-permute-done.51 = f32[256,512]{1,0:T(8,128)S(1)} collective-permute-done((f32[256,512]{1,0:T(8,128)S(1)}, f32[256,512]{1,0:T(8,128)S(1)}, u32[]{:S(2)}, u32[]{:S(2)}) %collective-permute-start.51) | collective-permute-done | bytes 524320 | tf_op jit(solution)/shard_map/ppermute | solution.py:440
  327.8 11.0 %collective-permute-done.50 = f32[256,512]{1,0:T(8,128)S(1)} collective-permute-done((f32[256,512]{1,0:T(8,128)S(1)}, f32[256,512]{1,0:T(8,128)S(1)}, u32[]{:S(2)}, u32[]{:S(2)}) %collective-permute-start.50) | collective-permute-done | bytes 524320 | tf_op jit(solution)/shard_map/ppermute | solution.py:440
  340.5 15.2 %collective-permute-done.41 = f32[192,512]{1,0:T(8,128)S(1)} collective-permute-done((f32[192,512]{1,0:T(8,128)S(1)}, f32[192,512]{1,0:T(8,128)S(1)}, u32[]{:S(2)}, u32[]{:S(2)}) %collective-permute-start.41) | collective-permute-done | bytes 393248 | tf_op jit(solution)/shard_map/ppermute | solution.py:440
  358.1 17.3 %collective-permute-done.53.refs_11_ = f32[256,512]{1,0:T(8,128)S(1)} collective-permute-done((f32[256,512]{1,0:T(8,128)S(1)}, f32[256,512]{1,0:T(8,128)S(1)}, u32[]{:S(2)}, u32[]{:S(2)}) %collective-permute-start.53) | collective-permute-done | bytes 524320 | tf_op jit(solution)/shard_map/ppermute | solution.py:440
  383.9 8.3 %collective-permute-done.43.refs_6_ = f32[192,512]{1,0:T(8,128)S(1)} collective-permute-done((f32[192,512]{1,0:T(8,128)S(1)}, f32[192,512]{1,0:T(8,128)S(1)}, u32[]{:S(2)}, u32[]{:S(2)}) %collective-permute-start.43) | collective-permute-done | bytes 393248 | tf_op jit(solution)/shard_map/ppermute | solution.py:440
  396.1 8.4 %collective-permute-done.35.refs_3_ = f32[192,512]{1,0:T(8,128)S(1)} collective-permute-done((f32[192,512]{1,0:T(8,128)S(1)}, f32[192,512]{1,0:T(8,128)S(1)}, u32[]{:S(2)}, u32[]{:S(2)}) %collective-permute-start.35) | collective-permute-done | bytes 393248 | tf_op jit(solution)/shard_map/ppermute | solution.py:440
  413.0 8.4 %collective-permute-done.45.refs_8_ = f32[192,512]{1,0:T(8,128)S(1)} collective-permute-done((f32[192,512]{1,0:T(8,128)S(1)}, f32[192,512]{1,0:T(8,128)S(1)}, u32[]{:S(2)}, u32[]{:S(2)}) %collective-permute-start.45) | collective-permute-done | bytes 393248 | tf_op jit(solution)/shard_map/ppermute | solution.py:440
  428.4 107.7 %factor.1 = f32[512,512]{1,0:T(8,128)} custom-call(s32[3]{0:T(128)} %pad_add_fusion.place_ref.me_ref, s32[8]{0:T(128)} %stack.123.order_ref, s32[344]{0:T(512)} %constant.28.table_ref, f32[192,512]{1,0:T(8,128)} %copy-done.14, f32[192,512]{1,0:T(8,128)} %copy-done.26, f32[192,512]{1,0:T(8,128)} %copy-done.28, f32[192,512]{1,0:T(8,128)} %copy-done.29, ...), custom_call_target="tpu_custom_call" | custom-call | flops 60000002048 | bytes 20000000 | tf_op jit(solution)/shard_map/factor/pallas_call | solution.py:205
  (187 shorter events, 141.8 us)
Async XLA Ops:
  1.2 47.6 %collective-permute-start.15 = (f32[512,512]{1,0:T(8,128)}, f32[512,512]{1,0:T(8,128)}, u32[]{:S(2)}, u32[]{:S(2)}) collective-permute-start(f32[512,512]{1,0:T(8,128)} %refs_14_.1), channel_id=1, source_target_pairs={{0,4},{2,6},{4,0},{6,2},{1,5},{3,7},{5,1},{7,3},{8,12},{10,14},{12... | collective-permute-start | bytes 3145736 | tf_op jit(solution)/shard_map/ppermute | solution.py:440
  2.4 48.5 %collective-permute-start.13 = (f32[512,512]{1,0:T(8,128)}, f32[512,512]{1,0:T(8,128)}, u32[]{:S(2)}, u32[]{:S(2)}) collective-permute-start(f32[512,512]{1,0:T(8,128)} %refs_14_.1), channel_id=1, source_target_pairs={{0,2},{2,0},{4,6},{6,4},{1,3},{3,1},{5,7},{7,5},{8,10},{10,8},{12,... | collective-permute-start | bytes 3145736 | tf_op jit(solution)/shard_map/ppermute | solution.py:440
  2.7 49.6 %collective-permute-start.12 = (f32[512,512]{1,0:T(8,128)}, f32[512,512]{1,0:T(8,128)}, u32[]{:S(2)}, u32[]{:S(2)}) collective-permute-start(f32[512,512]{1,0:T(8,128)} %refs_14_.1), channel_id=1, source_target_pairs={{0,1},{1,0},{2,3},{3,2},{4,5},{5,4},{6,7},{7,6},{8,9},{9,8},{10,11... | collective-permute-start | bytes 3145736 | tf_op jit(solution)/shard_map/ppermute | solution.py:440
  5.9 47.2 %collective-permute-start.3 = (f32[512,512]{1,0:T(8,128)S(1)}, f32[512,512]{1,0:T(8,128)S(1)}, u32[]{:S(2)}, u32[]{:S(2)}) collective-permute-start(f32[512,512]{1,0:T(8,128)S(1)} %get-tuple-element.25.refs_1_), channel_id=1, source_target_pairs={{8,0},{16,8},{24,16},{9,1},{17,9},{25,17},{10,2},{18,10},{26,18},{... | collective-permute-start | bytes 3145736 | tf_op jit(solution)/shard_map/ppermute | solution.py:468
  25.2 28.0 %collective-permute-start.1 = (f32[512,512]{1,0:T(8,128)S(1)}, f32[512,512]{1,0:T(8,128)S(1)}, u32[]{:S(2)}, u32[]{:S(2)}) collective-permute-start(f32[512,512]{1,0:T(8,128)S(1)} %get-tuple-element.25.refs_1_), channel_id=1, source_target_pairs={{0,8},{8,16},{16,24},{1,9},{9,17},{17,25},{2,10},{10,18},{18,26},{... | collective-permute-start | bytes 3145736 | tf_op jit(solution)/shard_map/ppermute | solution.py:468
  53.1 28.1 %collective-permute-start.16 = (f32[512,512]{1,0:T(8,128)}, f32[512,512]{1,0:T(8,128)S(1)}, u32[]{:S(2)}, u32[]{:S(2)}) collective-permute-start(f32[512,512]{1,0:T(8,128)} %collective-permute-done.15.refs_14_.refs_18_), channel_id=1, source_target_pairs={{0,1},{1,0},{2,3},{3,2},{4,5},{5,4},{6,7},{7,6},{8,9},{9,8},{10,11... | collective-permute-start | bytes 3145736 | tf_op jit(solution)/shard_map/ppermute | solution.py:440
  53.2 42.1 %collective-permute-start.7 = (f32[512,512]{1,0:T(8,128)S(1)}, f32[512,512]{1,0:T(8,128)}, u32[]{:S(2)}, u32[]{:S(2)}) collective-permute-start(f32[512,512]{1,0:T(8,128)S(1)} %collective-permute-done.3.refs_5_), channel_id=1, source_target_pairs={{8,0},{16,8},{24,16},{9,1},{17,9},{25,17},{10,2},{18,10},{26,18},{... | collective-permute-start | bytes 3145736 | tf_op jit(solution)/shard_map/ppermute | solution.py:468
  72.8 27.7 %collective-permute-start.5 = (f32[512,512]{1,0:T(8,128)S(1)}, f32[512,512]{1,0:T(8,128)}, u32[]{:S(2)}, u32[]{:S(2)}) collective-permute-start(f32[512,512]{1,0:T(8,128)S(1)} %collective-permute-done.1.refs_3_), channel_id=1, source_target_pairs={{0,8},{8,16},{16,24},{1,9},{9,17},{17,25},{2,10},{10,18},{18,26},{... | collective-permute-start | bytes 3145736 | tf_op jit(solution)/shard_map/ppermute | solution.py:468
  76.8 41.0 %collective-permute-start.6 = (f32[512,512]{1,0:T(8,128)S(1)}, f32[512,512]{1,0:T(8,128)}, u32[]{:S(2)}, u32[]{:S(2)}) collective-permute-start(f32[512,512]{1,0:T(8,128)S(1)} %collective-permute-done.2.refs_4_), channel_id=1, source_target_pairs={{8,0},{16,8},{24,16},{9,1},{17,9},{25,17},{10,2},{18,10},{26,18},{... | collective-permute-start | bytes 3145736 | tf_op jit(solution)/shard_map/ppermute | solution.py:468
  79.9 43.2 %collective-permute-start.4 = (f32[512,512]{1,0:T(8,128)S(1)}, f32[512,512]{1,0:T(8,128)}, u32[]{:S(2)}, u32[]{:S(2)}) collective-permute-start(f32[512,512]{1,0:T(8,128)S(1)} %collective-permute-done.refs_2_), channel_id=1, source_target_pairs={{0,8},{8,16},{16,24},{1,9},{9,17},{17,25},{2,10},{10,18},{18,26},{... | collective-permute-start | bytes 3145736 | tf_op jit(solution)/shard_map/ppermute | solution.py:468
  81.2 44.5 %collective-permute-start.14 = (f32[512,512]{1,0:T(8,128)}, f32[512,512]{1,0:T(8,128)}, u32[]{:S(2)}, u32[]{:S(2)}) collective-permute-start(f32[512,512]{1,0:T(8,128)} %collective-permute-done.13.refs_12_.refs_16_), channel_id=1, source_target_pairs={{0,1},{1,0},{2,3},{3,2},{4,5},{5,4},{6,7},{7,6},{8,9},{9,8},{10,11... | collective-permute-start | bytes 3145736 | tf_op jit(solution)/shard_map/ppermute | solution.py:440
  95.3 45.0 %collective-permute-start.11 = (f32[512,512]{1,0:T(8,128)}, f32[512,512]{1,0:T(8,128)}, u32[]{:S(2)}, u32[]{:S(2)}) collective-permute-start(f32[512,512]{1,0:T(8,128)} %collective-permute-done.7.refs_9_), channel_id=1, source_target_pairs={{8,0},{16,8},{24,16},{9,1},{17,9},{25,17},{10,2},{18,10},{26,18},{... | collective-permute-start | bytes 3145736 | tf_op jit(solution)/shard_map/ppermute | solution.py:468
  100.6 42.7 %collective-permute-start.9 = (f32[512,512]{1,0:T(8,128)}, f32[512,512]{1,0:T(8,128)}, u32[]{:S(2)}, u32[]{:S(2)}) collective-permute-start(f32[512,512]{1,0:T(8,128)} %collective-permute-done.5.refs_7_), channel_id=1, source_target_pairs={{0,8},{8,16},{16,24},{1,9},{9,17},{17,25},{2,10},{10,18},{18,26},{... | collective-permute-start | bytes 3145736 | tf_op jit(solution)/shard_map/ppermute | solution.py:468
  117.8 45.0 %collective-permute-start.10 = (f32[512,512]{1,0:T(8,128)}, f32[512,512]{1,0:T(8,128)}, u32[]{:S(2)}, u32[]{:S(2)}) collective-permute-start(f32[512,512]{1,0:T(8,128)} %collective-permute-done.6.refs_8_), channel_id=1, source_target_pairs={{8,0},{16,8},{24,16},{9,1},{17,9},{25,17},{10,2},{18,10},{26,18},{... | collective-permute-start | bytes 3145736 | tf_op jit(solution)/shard_map/ppermute | solution.py:468
  123.1 42.6 %collective-permute-start.8 = (f32[512,512]{1,0:T(8,128)}, f32[512,512]{1,0:T(8,128)}, u32[]{:S(2)}, u32[]{:S(2)}) collective-permute-start(f32[512,512]{1,0:T(8,128)} %collective-permute-done.4.refs_6_), channel_id=1, source_target_pairs={{0,8},{8,16},{16,24},{1,9},{9,17},{17,25},{2,10},{10,18},{18,26},{... | collective-permute-start | bytes 3145736 | tf_op jit(solution)/shard_map/ppermute | solution.py:468
  307.6 31.2 %collective-permute-start.50 = (f32[256,512]{1,0:T(8,128)S(1)}, f32[256,512]{1,0:T(8,128)S(1)}, u32[]{:S(2)}, u32[]{:S(2)}) collective-permute-start(f32[256,512]{1,0:T(8,128)S(1)} %get-tuple-element.27), channel_id=1, source_target_pairs={{0,2},{2,0},{4,6},{6,4},{1,3},{3,1},{5,7},{7,5},{8,10},{10,8},{12,... | collective-permute-start | bytes 1572872 | tf_op jit(solution)/shard_map/ppermute | solution.py:440
  319.4 36.5 %collective-permute-start.30 = (f32[192,512]{1,0:T(8,128)S(1)}, f32[192,512]{1,0:T(8,128)S(1)}, u32[]{:S(2)}, u32[]{:S(2)}) collective-permute-start(f32[192,512]{1,0:T(8,128)S(1)} %get-tuple-element.35), channel_id=1, source_target_pairs={{0,2},{2,0},{4,6},{6,4},{1,3},{3,1},{5,7},{7,5},{8,10},{10,8},{12,... | collective-permute-start | bytes 1179656 | tf_op jit(solution)/shard_map/ppermute | solution.py:440
  321.1 34.6 %collective-permute-start.41 = (f32[192,512]{1,0:T(8,128)S(1)}, f32[192,512]{1,0:T(8,128)S(1)}, u32[]{:S(2)}, u32[]{:S(2)}) collective-permute-start(f32[192,512]{1,0:T(8,128)S(1)} %get-tuple-element.34), channel_id=1, source_target_pairs={{0,2},{2,0},{4,6},{6,4},{1,3},{3,1},{5,7},{7,5},{8,10},{10,8},{12,... | collective-permute-start | bytes 1179656 | tf_op jit(solution)/shard_map/ppermute | solution.py:440
  327.6 28.3 %collective-permute-start.32 = (f32[192,512]{1,0:T(8,128)S(1)}, f32[192,512]{1,0:T(8,128)S(1)}, u32[]{:S(2)}, u32[]{:S(2)}) collective-permute-start(f32[192,512]{1,0:T(8,128)S(1)} %fusion.12), channel_id=1, source_target_pairs={{0,4},{2,6},{4,0},{6,2},{1,5},{3,7},{5,1},{7,3},{8,12},{10,14},{12... | collective-permute-start | bytes 1179656 | tf_op jit(solution)/shard_map/ppermute | solution.py:440
  338.8 36.6 %collective-permute-start.40 = (f32[192,512]{1,0:T(8,128)S(1)}, f32[192,512]{1,0:T(8,128)S(1)}, u32[]{:S(2)}, u32[]{:S(2)}) collective-permute-start(f32[192,512]{1,0:T(8,128)S(1)} %get-tuple-element.33), channel_id=1, source_target_pairs={{0,2},{2,0},{4,6},{6,4},{1,3},{3,1},{5,7},{7,5},{8,10},{10,8},{12,... | collective-permute-start | bytes 1179656 | tf_op jit(solution)/shard_map/ppermute | solution.py:440
  339.6 35.8 %collective-permute-start.53 = (f32[256,512]{1,0:T(8,128)S(1)}, f32[256,512]{1,0:T(8,128)S(1)}, u32[]{:S(2)}, u32[]{:S(2)}) collective-permute-start(f32[256,512]{1,0:T(8,128)S(1)} %fusion.2.refs_10_), channel_id=1, source_target_pairs={{0,2},{2,0},{4,6},{6,4},{1,3},{3,1},{5,7},{7,5},{8,10},{10,8},{12,... | collective-permute-start | bytes 1572872 | tf_op jit(solution)/shard_map/ppermute | solution.py:440
  357.4 34.9 %collective-permute-start.54 = (f32[256,512]{1,0:T(8,128)S(1)}, f32[256,512]{1,0:T(8,128)S(1)}, u32[]{:S(2)}, u32[]{:S(2)}) collective-permute-start(f32[256,512]{1,0:T(8,128)S(1)} %fusion.2.refs_10_), channel_id=1, source_target_pairs={{0,4},{2,6},{4,0},{6,2},{1,5},{3,7},{5,1},{7,3},{8,12},{10,14},{12... | collective-permute-start | bytes 1572872 | tf_op jit(solution)/shard_map/ppermute | solution.py:440
  392.3 29.1 %collective-permute-start.45 = (f32[192,512]{1,0:T(8,128)S(1)}, f32[192,512]{1,0:T(8,128)S(1)}, u32[]{:S(2)}, u32[]{:S(2)}) collective-permute-start(f32[192,512]{1,0:T(8,128)S(1)} %collective-permute-done.43.refs_6_), channel_id=1, source_target_pairs={{0,4},{2,6},{4,0},{6,2},{1,5},{3,7},{5,1},{7,3},{8,12},{10,14},{12... | collective-permute-start | bytes 1179656 | tf_op jit(solution)/shard_map/ppermute | solution.py:440
  394.4 33.9 %collective-permute-start.56 = (f32[4,256,512]{2,1,0:T(8,128)S(1)}, f32[4,256,512]{2,1,0:T(8,128)}, u32[]{:S(2)}, u32[]{:S(2)}) collective-permute-start(f32[4,256,512]{2,1,0:T(8,128)S(1)} %pad_maximum_fusion), channel_id=1, source_target_pairs={{0,1},{1,0},{2,3},{3,2},{4,5},{5,4},{6,7},{7,6},{8,9},{9,8},{10,11... | collective-permute-start | bytes 6291464 | tf_op jit(solution)/shard_map/ppermute | solution.py:440
  (65 other events, 1923.3 us)

commit v2 on v1

--- a/solution.py
+++ b/solution.py
@@ -97,7 +97,6 @@
 
 def factor_kernel(blocks, size, groups, bundles, shares, swaps, scale, extra, most, me_ref, order_ref, table_ref, *refs):
     per = blocks // groups
-    width = per * size
     arrays = shares + swaps
     g_refs = [refs[n * arrays:(n + 1) * arrays] for n in range(len(bundles))]
     refs = refs[len(bundles) * arrays:]
@@ -112,14 +111,12 @@
         for t in range(pieces):
             piece = arrays_in[t] if t < shares else arrays_in[shares + t // shares - 1].at[t % shares]
             first = 0
-            for s in bundle:
-                rows = (s + 1) * width // pieces
-                start = pl.multiple_of((me - s) * width + order_ref[t] * rows, 8)
-                for h in range(per):
-                    copies[s].append(pltpu.make_async_copy(
-                        piece.at[pl.ds(first, rows), pl.ds(h * size, size)],
-                        g.at[(me - s) * per + h, pl.ds(start, rows), :], sem.at[n_sem]))
-                    n_sem += 1
+            for (s, h), (top, at), n in segments(bundle, per):
+                rows = n * size // pieces
+                start = pl.multiple_of(((me - top) * per + at) * size + order_ref[t] * rows, 8)
+                copies[s].append(pltpu.make_async_copy(
+                    piece.at[pl.ds(first, rows), :], g.at[(me - s) * per + h, pl.ds(start, rows), :], sem.at[n_sem]))
+                n_sem += 1
                 first += rows
     for s in range(groups):
         for h in range(per):
@@ -213,7 +210,8 @@
             pltpu.VMEM((blocks + extra + 1, size, 3 * size), BF16),
             pltpu.VMEM((size, size), F32),
             pltpu.VMEM((size, size), F32),
-            pltpu.SemaphoreType.DMA((groups * per * (shares * (1 + swaps) + 1),)),
+            pltpu.SemaphoreType.DMA((
+                sum(len(segments(b, per)) for b in bundles) * shares * (1 + swaps) + groups * per,)),
         ],
         compiler_params=pltpu.CompilerParams(vmem_limit_bytes=56 * 1024 * 1024),
         cost_estimate=pl.CostEstimate(flops=6 * 10**10, bytes_accessed=2 * 10**7, transcendentals=0),
@@ -373,30 +371,56 @@
             each_out(z, m, lambda c: c.wait())
 
 
-def gram_kernel(bundle, sizes, per, place_ref, *refs):
+def segments(bundle, per):
+    runs = []
+    for s, h in bundle:
+        runs += [((s, before), (s, h), 1) for before in range(h)]
+        if h == per - 1:
+            runs.append(((s, h), (s, h), 1 + s * per))
+        else:
+            runs.append(((s, h), (s, h), 1))
+            if s:
+                runs.append(((s, h), (s - 1, 0), s * per))
+    return runs
+
+
+def gram_kernel(bundle, known, sizes, per, place_ref, *refs):
     cols_n, layers = sizes
     shares = cols_n * layers
-    n_p = (bundle[-1] + 1) * per
-    p_refs, outs, (left3, right3, g, sem) = refs[:n_p], refs[n_p:n_p + layers], refs[n_p + layers:]
+    top = max(s for s, _ in known)
+    p_refs, outs, (left3, right3, g, sem) = refs[:len(known)], refs[len(known):len(known) + layers], refs[len(known) + layers:]
     rows, size = p_refs[0].shape
-    width = size * per
     col, layer = place_ref[1], place_ref[2]
-    for t in range(bundle[-1] + 1):
-        for h in range(per):
-            hi, lo = split(p_refs[t * per + h][...])
-            here = pl.ds(h * size, size)
-            for n, part in enumerate((hi, hi, lo)):
-                left3[t, n * rows:(n + 1) * rows, here] = part
-            if t in bundle:
-                for n, part in enumerate((hi, lo, hi)):
-                    right3[bundle.index(t), n * rows:(n + 1) * rows, here] = part
+    runs = segments(bundle, per)
+    rights = sorted(set(run[0] for run in runs))
+
+    def at(t, h):
+        return (top - t) * per + h
+
+    for n, (t, h) in enumerate(known):
+        hi, lo = split(p_refs[n][...])
+        for m, part in enumerate((hi, hi, lo)):
+            left3[at(t, h), m * rows:(m + 1) * rows, :] = part
+        if (t, h) in rights:
+            for m, part in enumerate((hi, lo, hi)):
+                right3[rights.index((t, h)), m * rows:(m + 1) * rows, :] = part
     base, first = 0, 0
     copies = []
-    for i, s in enumerate(bundle):
-        for t in range(s, -1, -1):
-            at = base + (s - t) * width
-            g[at:at + width, :] = mm(left3[t], right3[i], TN)
-        n = (s + 1) * width // shares
+    for column, row, count in runs:
+        right, start = rights.index(column), at(*row)
+
+        together = count if len(bundle) == 1 else min(4, count)
+        if together == count:
+            for n in range(count):
+                g[base + n * size:base + (n + 1) * size, :] = mm(left3[start + n], right3[right], TN)
+        else:
+            @pl.loop(0, -(-count // together))
+            def _(step):
+                for k in range(together):
+                    n = jnp.minimum(step * together + k, count - 1)
+                    g[pl.ds(pl.multiple_of(base + n * size, size), size), :] = mm(left3[start + n], right3[right], TN)
+
+        n = count * size // shares
         for x in range(layers):
             for y in range(cols_n):
                 share = jnp.bitwise_xor(layer, x) * cols_n + jnp.bitwise_xor(col, y)
@@ -404,7 +428,7 @@
                 copies.append(pltpu.make_async_copy(
                     g.at[pl.ds(start, n), :], outs[x].at[y, pl.ds(first, n), :], sem.at[len(copies)]))
                 copies[-1].start()
-        base += (s + 1) * width
+        base += count * size
         first += n
     for c in copies:
         c.wait()
@@ -413,24 +437,25 @@
 def gram_call(place, bundle, panels, sizes):
     cols_n, layers = sizes
     per = len(panels[0])
-    rows, size = panels[0][0].shape
-    width = size * per
-    total = sum(s + 1 for s in bundle) * width
-    flat = sum(panels[:bundle[-1] + 1], [])
+    known = [(t, h) for t in range(len(panels)) for h in range(per) if (t, h) <= bundle[-1]]
+    flat = [panels[t][h] for t, h in known]
+    rows, size = flat[0].shape
+    runs = segments(bundle, per)
+    total = sum(run[2] for run in runs) * size
     vmem = pl.BlockSpec(memory_space=pltpu.VMEM)
     return pl.pallas_call(
-        functools.partial(gram_kernel, bundle, sizes, per),
-        out_shape=[jax.ShapeDtypeStruct((cols_n, total // (cols_n * layers), width), F32)] * layers,
+        functools.partial(gram_kernel, bundle, known, sizes, per),
+        out_shape=[jax.ShapeDtypeStruct((cols_n, total // (cols_n * layers), size), F32)] * layers,
         in_specs=[pl.BlockSpec(memory_space=pltpu.SMEM)] + [vmem] * len(flat),
         out_specs=[pl.BlockSpec(memory_space=pl.ANY)] * layers,
         scratch_shapes=[
-            pltpu.VMEM((bundle[-1] + 1, 3 * rows, width), BF16),
-            pltpu.VMEM((len(bundle), 3 * rows, width), BF16),
-            pltpu.VMEM((total, width), F32),
-            pltpu.SemaphoreType.DMA((len(bundle) * cols_n * layers,)),
+            pltpu.VMEM(((bundle[-1][0] + 1) * per, 3 * rows, size), BF16),
+            pltpu.VMEM((len(set(run[0] for run in runs)), 3 * rows, size), BF16),
+            pltpu.VMEM((total, size), F32),
+            pltpu.SemaphoreType.DMA((len(runs) * cols_n * layers,)),
         ],
         compiler_params=pltpu.CompilerParams(vmem_limit_bytes=48 * 1024 * 1024),
-        cost_estimate=pl.CostEstimate(flops=6 * total * width * rows, bytes_accessed=4 * total * width, transcendentals=0),
+        cost_estimate=pl.CostEstimate(flops=6 * total * size * rows, bytes_accessed=4 * total * size, transcendentals=0),
         name="gram",
     )(place, *flat)
 
@@ -497,24 +522,32 @@
         image = exchange_sum([images[x * per + h] for x in range(layers)], "layer")
         panels[0].append(exchange_sum([image[s] for s in range(cols_n)], "col", 1 + h % 2))
 
-    bundles = [[0, 1]] + [[s] for s in range(2, rows_n)]
+    bundles = all_bundles(rows_n, per)
     up = [(a, a + 1) for a in range(rows_n - 1)]
     g_arrays = []
-    for s in range(rows_n):
-        if s:
-            panels.append([lax.ppermute(part, "row", up) for part in panels[-1]])
-        for bundle in bundles:
-            if bundle[-1] == s:
-                gram = gram_call(place, bundle, panels, (cols_n, layers))
-                gram = exchange_sum(gram, "layer")
-                gram = [gram[y] for y in range(cols_n)]
-                gram = exchange_sum(gram, "col", 1)
-                pieces = own_and_others(gram, "col", 2)
-                g_arrays.append(pieces + own_and_others(jnp.stack(pieces), "layer")[1:])
+    for n, bundle in enumerate(bundles):
+        s = bundle[-1][0]
+        if s == len(panels):
+            panels.append([])
+            for h in range(per):
+                panels[-1].append(lax.ppermute(panels[-2][h], "row", up))
+        gram = gram_call(place, bundle, panels, (cols_n, layers))
+        gram = exchange_sum(gram, "layer")
+        gram = [gram[y] for y in range(cols_n)]
+        direct = n >= rows_n - 2
+        gram = exchange_sum(gram, "col", 0 if direct else 1)
+        pieces = own_and_others(gram, "col", 0 if direct else 2)
+        stack = jnp.stack(pieces)
+        g_arrays.append(pieces + own_and_others(stack, "layer")[1:])
     places = jnp.stack([(layer ^ x) * cols_n + (col ^ s) for x in range(layers) for s in range(cols_n)])
     return factor_apply(place, places, bundles, g_arrays, cols_n, panels, size, math.sqrt(order_m))
 
 
+def all_bundles(rows_n, per):
+    whole = [[(s, h) for h in range(per)] for s in range(rows_n - 1)]
+    return whole + [[(rows_n - 1, h)] for h in range(per)]
+
+
 def solution(mesh):
     placed = (P("row", "col"), P(("col", "layer"), "row"))
 

time: 537 us -> 529 us (0.985)
  the two profiles are of different devices: /device:TPU:29 before, /device:TPU:25 now
where the time goes in v2:
time: 529 us; the launch traced here: 528 us
  waiting for transfers between devices  241 us (46%)
  Pallas kernels  165 us (31%)
  starting transfers between devices  111 us (21%)
  other arithmetic  6.26 us (1%)
    ppermute x55, waiting for transfers between devices, shift_by_xor(): return lax.ppermute(x, axis, [(a, a ^ step) for a in range(n)])  148 us
    pallas_call x1, Pallas kernels, factor_apply(): pl.pallas_call(functools.partial(factor_kernel, blocks, size, groups, bun...  108 us
    ppermute x12, waiting for transfers between devices, chain(): got.append(lax.ppermute(got[-1], axis, pairs))  73.9 us
    ppermute x55, starting transfers between devices, shift_by_xor(): return lax.ppermute(x, axis, [(a, a ^ step) for a in range(n)])  72.3 us
    pallas_call x5, Pallas kernels, gram_call(): pl.pallas_call(functools.partial(gram_kernel, bundle, known, sizes, per),...  31.7 us
    ppermute x12, starting transfers between devices, chain(): got.append(lax.ppermute(got[-1], axis, pairs))  30.8 us
    pallas_call x2, Pallas kernels, image_call(): pl.pallas_call(functools.partial(image_kernel, sizes, cuts, per, last), o...  25.6 us
    ppermute x6, waiting for transfers between devices, shards(): panels[-1].append(lax.ppermute(panels[-2][h], 'row', up))  18.9 us
  transfers between devices with their start and end apart: 73, of which 37 were waited for; matrix products, arithmetic and copies ran while one was open for 2% of the time, Pallas kernels for 8%

profile of v2, /device:TPU:25, one launch (start us, length us, event | category | flops | bytes accessed | tf_op | source)
XLA Modules:
  0.0 528.2 jit_solution(15577915756246237564)
XLA Ops:
  8.1 17.1 %collective-permute-done.17.refs_16_.refs_20_ = f32[512,512]{1,0:T(8,128)S(1)} collective-permute-done((f32[512,512]{1,0:T(8,128)}, f32[512,512]{1,0:T(8,128)S(1)}, u32[]{:S(2)}, u32[]{:S(2)}) %collective-permute-start.17) | collective-permute-done | bytes 1048608 | tf_op jit(solution)/shard_map/ppermute | solution.py:465
  26.5 22.3 %collective-permute-done.15.refs_14_.refs_18_ = f32[512,512]{1,0:T(8,128)} collective-permute-done((f32[512,512]{1,0:T(8,128)}, f32[512,512]{1,0:T(8,128)}, u32[]{:S(2)}, u32[]{:S(2)}) %collective-permute-start.15) | collective-permute-done | bytes 1048608 | tf_op jit(solution)/shard_map/ppermute | solution.py:465
  58.4 14.4 %collective-permute-done.2.refs_4_ = f32[512,512]{1,0:T(8,128)S(1)} collective-permute-done((f32[512,512]{1,0:T(8,128)S(1)}, f32[512,512]{1,0:T(8,128)S(1)}, u32[]{:S(2)}, u32[]{:S(2)}) %collective-permute-start.2) | collective-permute-done | bytes 1048608 | tf_op jit(solution)/shard_map/ppermute | solution.py:493
  83.8 11.5 %collective-permute-done.7.refs_9_ = f32[512,512]{1,0:T(8,128)} collective-permute-done((f32[512,512]{1,0:T(8,128)S(1)}, f32[512,512]{1,0:T(8,128)}, u32[]{:S(2)}, u32[]{:S(2)}) %collective-permute-start.7) | collective-permute-done | bytes 1048608 | tf_op jit(solution)/shard_map/ppermute | solution.py:493
  101.8 16.0 %collective-permute-done.6.refs_8_ = f32[512,512]{1,0:T(8,128)} collective-permute-done((f32[512,512]{1,0:T(8,128)S(1)}, f32[512,512]{1,0:T(8,128)}, u32[]{:S(2)}, u32[]{:S(2)}) %collective-permute-start.6) | collective-permute-done | bytes 1048608 | tf_op jit(solution)/shard_map/ppermute | solution.py:493
  125.7 10.6 %inner.1.refs_22_ = f32[512,512]{1,0:T(8,128)} custom-call(s32[3]{0:T(128)} %pad_add_fusion.place_ref.me_ref, s32[8]{0:T(128)} %stack.162.s_place_ref, f32[512,512]{1,0:T(8,128)} %copy-done.10, f32[512,512]{1,0:T(8,128)} %copy-done.9, f32[512,512]{1,0:T(8,128)} %copy-done.17, f32[512,512]{1,0:T(8,128)} %copy-done.15, f32[512,512]{1,0:T(8,128)} %copy-done.16, ...), custom_call_target="tpu_custom_call" | custom-call | flops 4831838208 | bytes 8388608 | tf_op jit(solution)/shard_map/inner/pallas_call | solution.py:249
  143.2 19.6 %collective-permute-done.10.refs_12_ = f32[512,512]{1,0:T(8,128)} collective-permute-done((f32[512,512]{1,0:T(8,128)}, f32[512,512]{1,0:T(8,128)}, u32[]{:S(2)}, u32[]{:S(2)}) %collective-permute-start.10) | collective-permute-done | bytes 1048608 | tf_op jit(solution)/shard_map/ppermute | solution.py:493
  165.7 15.0 %image.1 = (f32[4,512,256]{2,1,0:T(8,128)}, f32[4,512,256]{2,1,0:T(8,128)}, f32[4,512,256]{2,1,0:T(8,128)}, f32[4,512,256]{2,1,0:T(8,128)}) custom-call(s32[3]{0:T(128)} %pad_add_fusion.place_ref.me_ref, s32[8]{0:T(128)} %stack.162.s_place_ref, f32[512,512]{1,0:T(8,128)} %copy-done.10, f32[512,512]{1,0:T(8,128)} %copy-done.9, f32[512,512]{1,0:T(8,128)} %copy-done.17, ...), custom_call_target="tpu_custom_call" | custom-call | flops 8053063680 | bytes 8388608 | tf_op jit(solution)/shard_map/image/pallas_call | solution.py:249
  193.0 9.9 %collective-permute-done.21 = f32[512,256]{1,0:T(8,128)S(1)} collective-permute-done((f32[512,256]{1,0:T(8,128)S(1)}, f32[512,256]{1,0:T(8,128)S(1)}, u32[]{:S(2)}, u32[]{:S(2)}) %collective-permute-start.21) | collective-permute-done | bytes 524320 | tf_op jit(solution)/shard_map/ppermute | solution.py:465
  206.1 8.0 %collective-permute-done.20 = f32[512,256]{1,0:T(8,128)S(1)} collective-permute-done((f32[512,256]{1,0:T(8,128)S(1)}, f32[512,256]{1,0:T(8,128)S(1)}, u32[]{:S(2)}, u32[]{:S(2)}) %collective-permute-start.20) | collective-permute-done | bytes 524320 | tf_op jit(solution)/shard_map/ppermute | solution.py:465
  215.9 9.8 %collective-permute-done.24 = f32[512,256]{1,0:T(8,128)S(1)} collective-permute-done((f32[512,256]{1,0:T(8,128)S(1)}, f32[512,256]{1,0:T(8,128)S(1)}, u32[]{:S(2)}, u32[]{:S(2)}) %collective-permute-start.24) | collective-permute-done | bytes 524320 | tf_op jit(solution)/shard_map/ppermute | solution.py:465
  228.5 10.4 %collective-permute-done.36.refs_3_.refs_28_ = f32[512,256]{1,0:T(8,128)S(1)} collective-permute-done((f32[512,256]{1,0:T(8,128)S(1)}, f32[512,256]{1,0:T(8,128)S(1)}, u32[]{:S(2)}, u32[]{:S(2)}) %collective-permute-start.36) | collective-permute-done | bytes 524320 | tf_op jit(solution)/shard_map/ppermute | solution.py:533
  240.3 6.3 %gram.6 = (f32[4,224,256]{2,1,0:T(8,128)S(1)}, f32[4,224,256]{2,1,0:T(8,128)S(1)}) custom-call(s32[3]{0:T(128)S(1)} %copy-done.2, f32[512,256]{1,0:T(8,128)S(1)} %fusion.5.refs_0_.refs_25_, f32[512,256]{1,0:T(8,128)S(1)} %fusion.2.refs_1_.refs_26_, f32[512,256]{1,0:T(8,128)S(1)} %collective-permute-done.35.refs_2_.refs_27_, ...), custom_call_target="tpu_custom_call" | custom-call | flops 1409286144 | bytes 1835008 | tf_op jit(solution)/shard_map/gram/pallas_call | solution.py:446
  246.7 6.7 %collective-permute-start.37 = (f32[4,224,256]{2,1,0:T(8,128)S(1)}, f32[4,224,256]{2,1,0:T(8,128)S(1)}, u32[]{:S(2)}, u32[]{:S(2)}) collective-permute-start(f32[4,224,256]{2,1,0:T(8,128)S(1)} %get-tuple-element.26), channel_id=1, source_target_pairs={{0,1},{1,0},{2,3},{3,2},{4,5},{5,4},{6,7},{7,6},{8,9},{9,8},{10,11... | collective-permute-start | bytes 2752520 | tf_op jit(solution)/shard_map/ppermute | solution.py:465
  261.3 9.6 %gram.7 = (f32[4,352,256]{2,1,0:T(8,128)S(1)}, f32[4,352,256]{2,1,0:T(8,128)S(1)}) custom-call(s32[3]{0:T(128)S(1)} %copy-done.2, f32[512,256]{1,0:T(8,128)S(1)} %fusion.5.refs_0_.refs_25_, f32[512,256]{1,0:T(8,128)S(1)} %fusion.2.refs_1_.refs_26_, f32[512,256]{1,0:T(8,128)S(1)} %collective-permute-done.35.refs_2_.refs_27_, ...), custom_call_target="tpu_custom_call" | custom-call | flops 2214592512 | bytes 2883584 | tf_op jit(solution)/shard_map/gram/pallas_call | solution.py:446
  279.7 5.8 %gram.8 = (f32[4,224,256]{2,1,0:T(8,128)S(1)}, f32[4,224,256]{2,1,0:T(8,128)S(1)}) custom-call(s32[3]{0:T(128)S(1)} %copy-done.2, f32[512,256]{1,0:T(8,128)S(1)} %fusion.5.refs_0_.refs_25_, f32[512,256]{1,0:T(8,128)S(1)} %fusion.2.refs_1_.refs_26_, f32[512,256]{1,0:T(8,128)S(1)} %collective-permute-done.35.refs_2_.refs_27_, ...), custom_call_target="tpu_custom_call" | custom-call | flops 1409286144 | bytes 1835008 | tf_op jit(solution)/shard_map/gram/pallas_call | solution.py:446
  286.2 5.6 %collective-permute-done.64.refs_7_.refs_32_ = f32[512,256]{1,0:T(8,128)S(1)} collective-permute-done((f32[512,256]{1,0:T(8,128)S(1)}, f32[512,256]{1,0:T(8,128)S(1)}, u32[]{:S(2)}, u32[]{:S(2)}) %collective-permute-start.64) | collective-permute-done | bytes 524320 | tf_op jit(solution)/shard_map/ppermute | solution.py:533
  291.8 6.3 %gram.9 = (f32[4,256,256]{2,1,0:T(8,128)S(1)}, f32[4,256,256]{2,1,0:T(8,128)}) custom-call(s32[3]{0:T(128)S(1)} %copy-done.2, f32[512,256]{1,0:T(8,128)S(1)} %fusion.5.refs_0_.refs_25_, f32[512,256]{1,0:T(8,128)S(1)} %fusion.2.refs_1_.refs_26_, f32[512,256]{1,0:T(8,128)S(1)} %collective-permute-done.35.refs_2_.refs_27_, ...), custom_call_target="tpu_custom_call" | custom-call | flops 1610612736 | bytes 2097152 | tf_op jit(solution)/shard_map/gram/pallas_call | solution.py:446
  317.0 7.6 %collective-permute-done.50 = f32[352,256]{1,0:T(8,128)S(1)} collective-permute-done((f32[352,256]{1,0:T(8,128)S(1)}, f32[352,256]{1,0:T(8,128)S(1)}, u32[]{:S(2)}, u32[]{:S(2)}) %collective-permute-start.50) | collective-permute-done | bytes 360480 | tf_op jit(solution)/shard_map/ppermute | solution.py:465
  347.1 11.2 %collective-permute-done.59 = f32[224,256]{1,0:T(8,128)S(1)} collective-permute-done((f32[224,256]{1,0:T(8,128)S(1)}, f32[224,256]{1,0:T(8,128)S(1)}, u32[]{:S(2)}, u32[]{:S(2)}) %collective-permute-start.59) | collective-permute-done | bytes 229408 | tf_op jit(solution)/shard_map/ppermute | solution.py:465
  358.5 6.2 %collective-permute-done.58 = f32[224,256]{1,0:T(8,128)S(1)} collective-permute-done((f32[224,256]{1,0:T(8,128)S(1)}, f32[224,256]{1,0:T(8,128)S(1)}, u32[]{:S(2)}, u32[]{:S(2)}) %collective-permute-start.58) | collective-permute-done | bytes 229408 | tf_op jit(solution)/shard_map/ppermute | solution.py:465
  373.4 9.1 %collective-permute-done.43.refs_8_ = f32[224,256]{1,0:T(8,128)S(1)} collective-permute-done((f32[224,256]{1,0:T(8,128)S(1)}, f32[224,256]{1,0:T(8,128)S(1)}, u32[]{:S(2)}, u32[]{:S(2)}) %collective-permute-start.43) | collective-permute-done | bytes 229408 | tf_op jit(solution)/shard_map/ppermute | solution.py:465
  389.4 6.3 %collective-permute-start.54 = (f32[4,352,256]{2,1,0:T(8,128)S(1)}, f32[4,352,256]{2,1,0:T(8,128)}, u32[]{:S(2)}, u32[]{:S(2)}) collective-permute-start(f32[4,352,256]{2,1,0:T(8,128)S(1)} %pad_maximum_fusion), channel_id=1, source_target_pairs={{0,1},{1,0},{2,3},{3,2},{4,5},{5,4},{6,7},{7,6},{8,9},{9,8},{10,11... | collective-permute-start | bytes 4325384 | tf_op jit(solution)/shard_map/ppermute | solution.py:465
  420.0 108.0 %factor.1 = f32[512,512]{1,0:T(8,128)} custom-call(s32[3]{0:T(128)} %pad_add_fusion.place_ref.me_ref, s32[8]{0:T(128)} %stack.153.order_ref, s32[344]{0:T(512)} %constant.28.table_ref, f32[96,256]{1,0:T(8,128)} %copy-done.23, f32[96,256]{1,0:T(8,128)} %copy-done.37, f32[96,256]{1,0:T(8,128)} %copy-done.36, f32[96,256]{1,0:T(8,128)} %copy-done.38, ...), custom_call_target="tpu_custom_call" | custom-call | flops 60000002048 | bytes 20000000 | tf_op jit(solution)/shard_map/factor/pallas_call | solution.py:202
  (242 shorter events, 173.8 us)
Async XLA Ops:
  2.2 46.6 %collective-permute-start.15 = (f32[512,512]{1,0:T(8,128)}, f32[512,512]{1,0:T(8,128)}, u32[]{:S(2)}, u32[]{:S(2)}) collective-permute-start(f32[512,512]{1,0:T(8,128)} %refs_14_.1), channel_id=1, source_target_pairs={{0,4},{2,6},{4,0},{6,2},{1,5},{3,7},{5,1},{7,3},{8,12},{10,14},{12... | collective-permute-start | bytes 3145736 | tf_op jit(solution)/shard_map/ppermute | solution.py:465
  2.4 48.5 %collective-permute-start.13 = (f32[512,512]{1,0:T(8,128)}, f32[512,512]{1,0:T(8,128)}, u32[]{:S(2)}, u32[]{:S(2)}) collective-permute-start(f32[512,512]{1,0:T(8,128)} %refs_14_.1), channel_id=1, source_target_pairs={{0,2},{2,0},{4,6},{6,4},{1,3},{3,1},{5,7},{7,5},{8,10},{10,8},{12,... | collective-permute-start | bytes 3145736 | tf_op jit(solution)/shard_map/ppermute | solution.py:465
  2.7 49.6 %collective-permute-start.12 = (f32[512,512]{1,0:T(8,128)}, f32[512,512]{1,0:T(8,128)}, u32[]{:S(2)}, u32[]{:S(2)}) collective-permute-start(f32[512,512]{1,0:T(8,128)} %refs_14_.1), channel_id=1, source_target_pairs={{0,1},{1,0},{2,3},{3,2},{4,5},{5,4},{6,7},{7,6},{8,9},{9,8},{10,11... | collective-permute-start | bytes 3145736 | tf_op jit(solution)/shard_map/ppermute | solution.py:465
  5.9 47.2 %collective-permute-start.3 = (f32[512,512]{1,0:T(8,128)S(1)}, f32[512,512]{1,0:T(8,128)S(1)}, u32[]{:S(2)}, u32[]{:S(2)}) collective-permute-start(f32[512,512]{1,0:T(8,128)S(1)} %get-tuple-element.33.refs_1_), channel_id=1, source_target_pairs={{8,0},{16,8},{24,16},{9,1},{17,9},{25,17},{10,2},{18,10},{26,18},{... | collective-permute-start | bytes 3145736 | tf_op jit(solution)/shard_map/ppermute | solution.py:493
  25.2 28.0 %collective-permute-start.1 = (f32[512,512]{1,0:T(8,128)S(1)}, f32[512,512]{1,0:T(8,128)S(1)}, u32[]{:S(2)}, u32[]{:S(2)}) collective-permute-start(f32[512,512]{1,0:T(8,128)S(1)} %get-tuple-element.33.refs_1_), channel_id=1, source_target_pairs={{0,8},{8,16},{16,24},{1,9},{9,17},{17,25},{2,10},{10,18},{18,26},{... | collective-permute-start | bytes 3145736 | tf_op jit(solution)/shard_map/ppermute | solution.py:493
  50.9 25.8 %collective-permute-start = (f32[512,512]{1,0:T(8,128)S(1)}, f32[512,512]{1,0:T(8,128)S(1)}, u32[]{:S(2)}, u32[]{:S(2)}) collective-permute-start(f32[512,512]{1,0:T(8,128)S(1)} %get-tuple-element.34.refs_0_), channel_id=1, source_target_pairs={{0,8},{8,16},{16,24},{1,9},{9,17},{17,25},{2,10},{10,18},{18,26},{... | collective-permute-start | bytes 3145736 | tf_op jit(solution)/shard_map/ppermute | solution.py:493
  52.2 27.6 %collective-permute-start.18 = (f32[512,512]{1,0:T(8,128)S(1)}, f32[512,512]{1,0:T(8,128)S(1)}, u32[]{:S(2)}, u32[]{:S(2)}) collective-permute-start(f32[512,512]{1,0:T(8,128)S(1)} %collective-permute-done.17.refs_16_.refs_20_), channel_id=1, source_target_pairs={{0,1},{1,0},{2,3},{3,2},{4,5},{5,4},{6,7},{7,6},{8,9},{9,8},{10,11... | collective-permute-start | bytes 3145736 | tf_op jit(solution)/shard_map/ppermute | solution.py:465
  53.1 28.1 %collective-permute-start.16 = (f32[512,512]{1,0:T(8,128)}, f32[512,512]{1,0:T(8,128)S(1)}, u32[]{:S(2)}, u32[]{:S(2)}) collective-permute-start(f32[512,512]{1,0:T(8,128)} %collective-permute-done.15.refs_14_.refs_18_), channel_id=1, source_target_pairs={{0,1},{1,0},{2,3},{3,2},{4,5},{5,4},{6,7},{7,6},{8,9},{9,8},{10,11... | collective-permute-start | bytes 3145736 | tf_op jit(solution)/shard_map/ppermute | solution.py:465
  53.2 42.1 %collective-permute-start.7 = (f32[512,512]{1,0:T(8,128)S(1)}, f32[512,512]{1,0:T(8,128)}, u32[]{:S(2)}, u32[]{:S(2)}) collective-permute-start(f32[512,512]{1,0:T(8,128)S(1)} %collective-permute-done.3.refs_5_), channel_id=1, source_target_pairs={{8,0},{16,8},{24,16},{9,1},{17,9},{25,17},{10,2},{18,10},{26,18},{... | collective-permute-start | bytes 3145736 | tf_op jit(solution)/shard_map/ppermute | solution.py:493
  72.8 27.6 %collective-permute-start.5 = (f32[512,512]{1,0:T(8,128)S(1)}, f32[512,512]{1,0:T(8,128)}, u32[]{:S(2)}, u32[]{:S(2)}) collective-permute-start(f32[512,512]{1,0:T(8,128)S(1)} %collective-permute-done.1.refs_3_), channel_id=1, source_target_pairs={{0,8},{8,16},{16,24},{1,9},{9,17},{17,25},{2,10},{10,18},{18,26},{... | collective-permute-start | bytes 3145736 | tf_op jit(solution)/shard_map/ppermute | solution.py:493
  76.8 41.0 %collective-permute-start.6 = (f32[512,512]{1,0:T(8,128)S(1)}, f32[512,512]{1,0:T(8,128)}, u32[]{:S(2)}, u32[]{:S(2)}) collective-permute-start(f32[512,512]{1,0:T(8,128)S(1)} %collective-permute-done.2.refs_4_), channel_id=1, source_target_pairs={{8,0},{16,8},{24,16},{9,1},{17,9},{25,17},{10,2},{18,10},{26,18},{... | collective-permute-start | bytes 3145736 | tf_op jit(solution)/shard_map/ppermute | solution.py:493
  79.9 43.2 %collective-permute-start.4 = (f32[512,512]{1,0:T(8,128)S(1)}, f32[512,512]{1,0:T(8,128)}, u32[]{:S(2)}, u32[]{:S(2)}) collective-permute-start(f32[512,512]{1,0:T(8,128)S(1)} %collective-permute-done.refs_2_), channel_id=1, source_target_pairs={{0,8},{8,16},{16,24},{1,9},{9,17},{17,25},{2,10},{10,18},{18,26},{... | collective-permute-start | bytes 3145736 | tf_op jit(solution)/shard_map/ppermute | solution.py:493
  81.2 44.5 %collective-permute-start.14 = (f32[512,512]{1,0:T(8,128)}, f32[512,512]{1,0:T(8,128)}, u32[]{:S(2)}, u32[]{:S(2)}) collective-permute-start(f32[512,512]{1,0:T(8,128)} %collective-permute-done.13.refs_12_.refs_16_), channel_id=1, source_target_pairs={{0,1},{1,0},{2,3},{3,2},{4,5},{5,4},{6,7},{7,6},{8,9},{9,8},{10,11... | collective-permute-start | bytes 3145736 | tf_op jit(solution)/shard_map/ppermute | solution.py:465
  95.3 45.0 %collective-permute-start.11 = (f32[512,512]{1,0:T(8,128)}, f32[512,512]{1,0:T(8,128)}, u32[]{:S(2)}, u32[]{:S(2)}) collective-permute-start(f32[512,512]{1,0:T(8,128)} %collective-permute-done.7.refs_9_), channel_id=1, source_target_pairs={{8,0},{16,8},{24,16},{9,1},{17,9},{25,17},{10,2},{18,10},{26,18},{... | collective-permute-start | bytes 3145736 | tf_op jit(solution)/shard_map/ppermute | solution.py:493
  100.5 42.7 %collective-permute-start.9 = (f32[512,512]{1,0:T(8,128)}, f32[512,512]{1,0:T(8,128)}, u32[]{:S(2)}, u32[]{:S(2)}) collective-permute-start(f32[512,512]{1,0:T(8,128)} %collective-permute-done.5.refs_7_), channel_id=1, source_target_pairs={{0,8},{8,16},{16,24},{1,9},{9,17},{17,25},{2,10},{10,18},{18,26},{... | collective-permute-start | bytes 3145736 | tf_op jit(solution)/shard_map/ppermute | solution.py:493
  117.8 45.0 %collective-permute-start.10 = (f32[512,512]{1,0:T(8,128)}, f32[512,512]{1,0:T(8,128)}, u32[]{:S(2)}, u32[]{:S(2)}) collective-permute-start(f32[512,512]{1,0:T(8,128)} %collective-permute-done.6.refs_8_), channel_id=1, source_target_pairs={{8,0},{16,8},{24,16},{9,1},{17,9},{25,17},{10,2},{18,10},{26,18},{... | collective-permute-start | bytes 3145736 | tf_op jit(solution)/shard_map/ppermute | solution.py:493
  123.1 42.6 %collective-permute-start.8 = (f32[512,512]{1,0:T(8,128)}, f32[512,512]{1,0:T(8,128)}, u32[]{:S(2)}, u32[]{:S(2)}) collective-permute-start(f32[512,512]{1,0:T(8,128)} %collective-permute-done.4.refs_6_), channel_id=1, source_target_pairs={{0,8},{8,16},{16,24},{1,9},{9,17},{17,25},{2,10},{10,18},{18,26},{... | collective-permute-start | bytes 3145736 | tf_op jit(solution)/shard_map/ppermute | solution.py:493
  227.2 29.9 %collective-permute-start.45 = (f32[512,256]{1,0:T(8,128)S(1)}, f32[512,256]{1,0:T(8,128)S(1)}, u32[]{:S(2)}, u32[]{:S(2)}) collective-permute-start(f32[512,256]{1,0:T(8,128)S(1)} %collective-permute-done.35.refs_2_.refs_27_), channel_id=1, source_target_pairs={{0,8},{8,16},{16,24},{1,9},{9,17},{17,25},{2,10},{10,18},{18,26},{... | collective-permute-start | bytes 1572872 | tf_op jit(solution)/shard_map/ppermute | solution.py:533
  246.7 31.3 %collective-permute-start.37 = (f32[4,224,256]{2,1,0:T(8,128)S(1)}, f32[4,224,256]{2,1,0:T(8,128)S(1)}, u32[]{:S(2)}, u32[]{:S(2)}) collective-permute-start(f32[4,224,256]{2,1,0:T(8,128)S(1)} %get-tuple-element.26), channel_id=1, source_target_pairs={{0,1},{1,0},{2,3},{3,2},{4,5},{5,4},{6,7},{7,6},{8,9},{9,8},{10,11... | collective-permute-start | bytes 2752520 | tf_op jit(solution)/shard_map/ppermute | solution.py:465
  270.9 35.4 %collective-permute-start.47 = (f32[4,352,256]{2,1,0:T(8,128)S(1)}, f32[4,352,256]{2,1,0:T(8,128)S(1)}, u32[]{:S(2)}, u32[]{:S(2)}) collective-permute-start(f32[4,352,256]{2,1,0:T(8,128)S(1)} %get-tuple-element.28), channel_id=1, source_target_pairs={{0,1},{1,0},{2,3},{3,2},{4,5},{5,4},{6,7},{7,6},{8,9},{9,8},{10,11... | collective-permute-start | bytes 4325384 | tf_op jit(solution)/shard_map/ppermute | solution.py:465
  328.4 36.7 %collective-permute-start.53 = (f32[352,256]{1,0:T(8,128)S(1)}, f32[352,256]{1,0:T(8,128)S(1)}, u32[]{:S(2)}, u32[]{:S(2)}) collective-permute-start(f32[352,256]{1,0:T(8,128)S(1)} %fusion.8.refs_10_), channel_id=1, source_target_pairs={{0,6},{2,4},{4,2},{6,0},{1,7},{3,5},{5,3},{7,1},{8,14},{10,12},{12... | collective-permute-start | bytes 1081352 | tf_op jit(solution)/shard_map/ppermute | solution.py:465
  333.4 33.4 %collective-permute-start.52 = (f32[352,256]{1,0:T(8,128)S(1)}, f32[352,256]{1,0:T(8,128)S(1)}, u32[]{:S(2)}, u32[]{:S(2)}) collective-permute-start(f32[352,256]{1,0:T(8,128)S(1)} %fusion.8.refs_10_), channel_id=1, source_target_pairs={{0,4},{2,6},{4,0},{6,2},{1,5},{3,7},{5,1},{7,3},{8,12},{10,14},{12... | collective-permute-start | bytes 1081352 | tf_op jit(solution)/shard_map/ppermute | solution.py:465
  367.2 29.4 %collective-permute-start.69 = (f32[256,256]{1,0:T(8,128)S(1)}, f32[256,256]{1,0:T(8,128)S(1)}, u32[]{:S(2)}, u32[]{:S(2)}) collective-permute-start(f32[256,256]{1,0:T(8,128)S(1)} %fusion.11.refs_20_), channel_id=1, source_target_pairs={{0,2},{2,0},{4,6},{6,4},{1,3},{3,1},{5,7},{7,5},{8,10},{10,8},{12,... | collective-permute-start | bytes 786440 | tf_op jit(solution)/shard_map/ppermute | solution.py:465
  389.4 30.6 %collective-permute-start.54 = (f32[4,352,256]{2,1,0:T(8,128)S(1)}, f32[4,352,256]{2,1,0:T(8,128)}, u32[]{:S(2)}, u32[]{:S(2)}) collective-permute-start(f32[4,352,256]{2,1,0:T(8,128)S(1)} %pad_maximum_fusion), channel_id=1, source_target_pairs={{0,1},{1,0},{2,3},{3,2},{4,5},{5,4},{6,7},{7,6},{8,9},{9,8},{10,11... | collective-permute-start | bytes 4325384 | tf_op jit(solution)/shard_map/ppermute | solution.py:465
  (88 other events, 2249.4 us)

commit v3 on v2

--- a/solution.py
+++ b/solution.py
@@ -534,9 +534,8 @@
         gram = gram_call(place, bundle, panels, (cols_n, layers))
         gram = exchange_sum(gram, "layer")
         gram = [gram[y] for y in range(cols_n)]
-        direct = n >= rows_n - 2
-        gram = exchange_sum(gram, "col", 0 if direct else 1)
-        pieces = own_and_others(gram, "col", 0 if direct else 2)
+        gram = exchange_sum(gram, "col", 0 if n >= rows_n - 2 else 1)
+        pieces = own_and_others(gram, "col", 0 if n > rows_n - 1 else 1 + n % 2)
         stack = jnp.stack(pieces)
         g_arrays.append(pieces + own_and_others(stack, "layer")[1:])
     places = jnp.stack([(layer ^ x) * cols_n + (col ^ s) for x in range(layers) for s in range(cols_n)])

time: 529 us -> 526 us (level)
    ppermute x55, waiting for transfers between devices: 148 us -> 142 us  [shift_by_xor(): return lax.ppermute(x, axis, [(a, a ^ step) for a in range(n)])]
  transfers between devices with their start and end apart: 73 -> 73, of which waited for: 37 -> 35; matrix products, arithmetic and copies ran while one was open for 2% -> 2% of each run, Pallas kernels for 8% -> 8%
where the time goes in v3:
time: 526 us; the launch traced here: 525 us
  waiting for transfers between devices  240 us (46%)
  Pallas kernels  165 us (31%)
  starting transfers between devices  109 us (21%)
  other arithmetic  6.27 us (1%)
    ppermute x55, waiting for transfers between devices, shift_by_xor(): return lax.ppermute(x, axis, [(a, a ^ step) for a in range(n)])  142 us
    pallas_call x1, Pallas kernels, factor_apply(): pl.pallas_call(functools.partial(factor_kernel, blocks, size, groups, bun...  108 us
    ppermute x12, waiting for transfers between devices, chain(): got.append(lax.ppermute(got[-1], axis, pairs))  73.9 us
    ppermute x55, starting transfers between devices, shift_by_xor(): return lax.ppermute(x, axis, [(a, a ^ step) for a in range(n)])  70.2 us
    pallas_call x5, Pallas kernels, gram_call(): pl.pallas_call(functools.partial(gram_kernel, bundle, known, sizes, per),...  31.7 us
    ppermute x12, starting transfers between devices, chain(): got.append(lax.ppermute(got[-1], axis, pairs))  30.8 us
    pallas_call x2, Pallas kernels, image_call(): pl.pallas_call(functools.partial(image_kernel, sizes, cuts, per, last), o...  25.6 us
    ppermute x6, waiting for transfers between devices, shards(): panels[-1].append(lax.ppermute(panels[-2][h], 'row', up))  24 us
  transfers between devices with their start and end apart: 73, of which 35 were waited for; matrix products, arithmetic and copies ran while one was open for 2% of the time, Pallas kernels for 8%

profile of v3, /device:TPU:25, one launch (start us, length us, event | category | flops | bytes accessed | tf_op | source)
XLA Modules:
  0.0 525.1 jit_solution(14335505536100901193)
XLA Ops:
  8.1 17.1 %collective-permute-done.17.refs_16_.refs_20_ = f32[512,512]{1,0:T(8,128)S(1)} collective-permute-done((f32[512,512]{1,0:T(8,128)}, f32[512,512]{1,0:T(8,128)S(1)}, u32[]{:S(2)}, u32[]{:S(2)}) %collective-permute-start.17) | collective-permute-done | bytes 1048608 | tf_op jit(solution)/shard_map/ppermute | solution.py:465
  26.5 22.3 %collective-permute-done.15.refs_14_.refs_18_ = f32[512,512]{1,0:T(8,128)} collective-permute-done((f32[512,512]{1,0:T(8,128)}, f32[512,512]{1,0:T(8,128)}, u32[]{:S(2)}, u32[]{:S(2)}) %collective-permute-start.15) | collective-permute-done | bytes 1048608 | tf_op jit(solution)/shard_map/ppermute | solution.py:465
  58.4 14.4 %collective-permute-done.2.refs_4_ = f32[512,512]{1,0:T(8,128)S(1)} collective-permute-done((f32[512,512]{1,0:T(8,128)S(1)}, f32[512,512]{1,0:T(8,128)S(1)}, u32[]{:S(2)}, u32[]{:S(2)}) %collective-permute-start.2) | collective-permute-done | bytes 1048608 | tf_op jit(solution)/shard_map/ppermute | solution.py:493
  83.8 11.5 %collective-permute-done.7.refs_9_ = f32[512,512]{1,0:T(8,128)} collective-permute-done((f32[512,512]{1,0:T(8,128)S(1)}, f32[512,512]{1,0:T(8,128)}, u32[]{:S(2)}, u32[]{:S(2)}) %collective-permute-start.7) | collective-permute-done | bytes 1048608 | tf_op jit(solution)/shard_map/ppermute | solution.py:493
  101.8 16.0 %collective-permute-done.6.refs_8_ = f32[512,512]{1,0:T(8,128)} collective-permute-done((f32[512,512]{1,0:T(8,128)S(1)}, f32[512,512]{1,0:T(8,128)}, u32[]{:S(2)}, u32[]{:S(2)}) %collective-permute-start.6) | collective-permute-done | bytes 1048608 | tf_op jit(solution)/shard_map/ppermute | solution.py:493
  125.7 10.6 %inner.1.refs_22_ = f32[512,512]{1,0:T(8,128)} custom-call(s32[3]{0:T(128)} %pad_add_fusion.place_ref.me_ref, s32[8]{0:T(128)} %stack.162.s_place_ref, f32[512,512]{1,0:T(8,128)} %copy-done.10, f32[512,512]{1,0:T(8,128)} %copy-done.9, f32[512,512]{1,0:T(8,128)} %copy-done.17, f32[512,512]{1,0:T(8,128)} %copy-done.15, f32[512,512]{1,0:T(8,128)} %copy-done.16, ...), custom_call_target="tpu_custom_call" | custom-call | flops 4831838208 | bytes 8388608 | tf_op jit(solution)/shard_map/inner/pallas_call | solution.py:249
  143.2 19.6 %collective-permute-done.10.refs_12_ = f32[512,512]{1,0:T(8,128)} collective-permute-done((f32[512,512]{1,0:T(8,128)}, f32[512,512]{1,0:T(8,128)}, u32[]{:S(2)}, u32[]{:S(2)}) %collective-permute-start.10) | collective-permute-done | bytes 1048608 | tf_op jit(solution)/shard_map/ppermute | solution.py:493
  165.7 15.0 %image.1 = (f32[4,512,256]{2,1,0:T(8,128)}, f32[4,512,256]{2,1,0:T(8,128)}, f32[4,512,256]{2,1,0:T(8,128)}, f32[4,512,256]{2,1,0:T(8,128)}) custom-call(s32[3]{0:T(128)} %pad_add_fusion.place_ref.me_ref, s32[8]{0:T(128)} %stack.162.s_place_ref, f32[512,512]{1,0:T(8,128)} %copy-done.10, f32[512,512]{1,0:T(8,128)} %copy-done.9, f32[512,512]{1,0:T(8,128)} %copy-done.17, ...), custom_call_target="tpu_custom_call" | custom-call | flops 8053063680 | bytes 8388608 | tf_op jit(solution)/shard_map/image/pallas_call | solution.py:249
  193.0 9.9 %collective-permute-done.21 = f32[512,256]{1,0:T(8,128)S(1)} collective-permute-done((f32[512,256]{1,0:T(8,128)S(1)}, f32[512,256]{1,0:T(8,128)S(1)}, u32[]{:S(2)}, u32[]{:S(2)}) %collective-permute-start.21) | collective-permute-done | bytes 524320 | tf_op jit(solution)/shard_map/ppermute | solution.py:465
  206.1 8.0 %collective-permute-done.20 = f32[512,256]{1,0:T(8,128)S(1)} collective-permute-done((f32[512,256]{1,0:T(8,128)S(1)}, f32[512,256]{1,0:T(8,128)S(1)}, u32[]{:S(2)}, u32[]{:S(2)}) %collective-permute-start.20) | collective-permute-done | bytes 524320 | tf_op jit(solution)/shard_map/ppermute | solution.py:465
  215.9 9.8 %collective-permute-done.24 = f32[512,256]{1,0:T(8,128)S(1)} collective-permute-done((f32[512,256]{1,0:T(8,128)S(1)}, f32[512,256]{1,0:T(8,128)S(1)}, u32[]{:S(2)}, u32[]{:S(2)}) %collective-permute-start.24) | collective-permute-done | bytes 524320 | tf_op jit(solution)/shard_map/ppermute | solution.py:465
  228.5 10.4 %collective-permute-done.36.refs_3_.refs_28_ = f32[512,256]{1,0:T(8,128)S(1)} collective-permute-done((f32[512,256]{1,0:T(8,128)S(1)}, f32[512,256]{1,0:T(8,128)S(1)}, u32[]{:S(2)}, u32[]{:S(2)}) %collective-permute-start.36) | collective-permute-done | bytes 524320 | tf_op jit(solution)/shard_map/ppermute | solution.py:533
  240.1 6.3 %gram.6 = (f32[4,224,256]{2,1,0:T(8,128)S(1)}, f32[4,224,256]{2,1,0:T(8,128)S(1)}) custom-call(s32[3]{0:T(128)S(1)} %copy-done.2, f32[512,256]{1,0:T(8,128)S(1)} %fusion.5.refs_0_.refs_25_, f32[512,256]{1,0:T(8,128)S(1)} %fusion.2.refs_1_.refs_26_, f32[512,256]{1,0:T(8,128)S(1)} %collective-permute-done.35.refs_2_.refs_27_, ...), custom_call_target="tpu_custom_call" | custom-call | flops 1409286144 | bytes 1835008 | tf_op jit(solution)/shard_map/gram/pallas_call | solution.py:446
  246.5 6.7 %collective-permute-start.37 = (f32[4,224,256]{2,1,0:T(8,128)S(1)}, f32[4,224,256]{2,1,0:T(8,128)S(1)}, u32[]{:S(2)}, u32[]{:S(2)}) collective-permute-start(f32[4,224,256]{2,1,0:T(8,128)S(1)} %get-tuple-element.26), channel_id=1, source_target_pairs={{0,1},{1,0},{2,3},{3,2},{4,5},{5,4},{6,7},{7,6},{8,9},{9,8},{10,11... | collective-permute-start | bytes 2752520 | tf_op jit(solution)/shard_map/ppermute | solution.py:465
  254.6 6.7 %collective-permute-done.46.refs_5_.refs_30_ = f32[512,256]{1,0:T(8,128)S(1)} collective-permute-done((f32[512,256]{1,0:T(8,128)S(1)}, f32[512,256]{1,0:T(8,128)S(1)}, u32[]{:S(2)}, u32[]{:S(2)}) %collective-permute-start.46) | collective-permute-done | bytes 524320 | tf_op jit(solution)/shard_map/ppermute | solution.py:533
  261.3 9.6 %gram.7 = (f32[4,352,256]{2,1,0:T(8,128)S(1)}, f32[4,352,256]{2,1,0:T(8,128)S(1)}) custom-call(s32[3]{0:T(128)S(1)} %copy-done.2, f32[512,256]{1,0:T(8,128)S(1)} %fusion.5.refs_0_.refs_25_, f32[512,256]{1,0:T(8,128)S(1)} %fusion.2.refs_1_.refs_26_, f32[512,256]{1,0:T(8,128)S(1)} %collective-permute-done.35.refs_2_.refs_27_, ...), custom_call_target="tpu_custom_call" | custom-call | flops 2214592512 | bytes 2883584 | tf_op jit(solution)/shard_map/gram/pallas_call | solution.py:446
  270.9 6.7 %collective-permute-start.47 = (f32[4,352,256]{2,1,0:T(8,128)S(1)}, f32[4,352,256]{2,1,0:T(8,128)S(1)}, u32[]{:S(2)}, u32[]{:S(2)}) collective-permute-start(f32[4,352,256]{2,1,0:T(8,128)S(1)} %get-tuple-element.28), channel_id=1, source_target_pairs={{0,1},{1,0},{2,3},{3,2},{4,5},{5,4},{6,7},{7,6},{8,9},{9,8},{10,11... | collective-permute-start | bytes 4325384 | tf_op jit(solution)/shard_map/ppermute | solution.py:465
  283.2 5.8 %gram.8 = (f32[4,224,256]{2,1,0:T(8,128)S(1)}, f32[4,224,256]{2,1,0:T(8,128)S(1)}) custom-call(s32[3]{0:T(128)S(1)} %copy-done.2, f32[512,256]{1,0:T(8,128)S(1)} %fusion.5.refs_0_.refs_25_, f32[512,256]{1,0:T(8,128)S(1)} %fusion.2.refs_1_.refs_26_, f32[512,256]{1,0:T(8,128)S(1)} %collective-permute-done.35.refs_2_.refs_27_, ...), custom_call_target="tpu_custom_call" | custom-call | flops 1409286144 | bytes 1835008 | tf_op jit(solution)/shard_map/gram/pallas_call | solution.py:446
  289.2 6.9 %collective-permute-done.64.refs_7_.refs_32_ = f32[512,256]{1,0:T(8,128)S(1)} collective-permute-done((f32[512,256]{1,0:T(8,128)S(1)}, f32[512,256]{1,0:T(8,128)S(1)}, u32[]{:S(2)}, u32[]{:S(2)}) %collective-permute-start.64) | collective-permute-done | bytes 524320 | tf_op jit(solution)/shard_map/ppermute | solution.py:533
  296.2 6.3 %gram.9 = (f32[4,256,256]{2,1,0:T(8,128)S(1)}, f32[4,256,256]{2,1,0:T(8,128)}) custom-call(s32[3]{0:T(128)S(1)} %copy-done.2, f32[512,256]{1,0:T(8,128)S(1)} %fusion.5.refs_0_.refs_25_, f32[512,256]{1,0:T(8,128)S(1)} %fusion.2.refs_1_.refs_26_, f32[512,256]{1,0:T(8,128)S(1)} %collective-permute-done.35.refs_2_.refs_27_, ...), custom_call_target="tpu_custom_call" | custom-call | flops 1610612736 | bytes 2097152 | tf_op jit(solution)/shard_map/gram/pallas_call | solution.py:446
  316.0 7.8 %collective-permute-done.48 = f32[352,256]{1,0:T(8,128)S(1)} collective-permute-done((f32[352,256]{1,0:T(8,128)S(1)}, f32[352,256]{1,0:T(8,128)S(1)}, u32[]{:S(2)}, u32[]{:S(2)}) %collective-permute-start.48) | collective-permute-done | bytes 360480 | tf_op jit(solution)/shard_map/ppermute | solution.py:465
  325.0 7.6 %collective-permute-done.50 = f32[352,256]{1,0:T(8,128)S(1)} collective-permute-done((f32[352,256]{1,0:T(8,128)S(1)}, f32[352,256]{1,0:T(8,128)S(1)}, u32[]{:S(2)}, u32[]{:S(2)}) %collective-permute-start.50) | collective-permute-done | bytes 360480 | tf_op jit(solution)/shard_map/ppermute | solution.py:465
  346.5 11.2 %collective-permute-done.41.refs_6_ = f32[224,256]{1,0:T(8,128)S(1)} collective-permute-done((f32[224,256]{1,0:T(8,128)S(1)}, f32[224,256]{1,0:T(8,128)S(1)}, u32[]{:S(2)}, u32[]{:S(2)}) %collective-permute-start.41) | collective-permute-done | bytes 229408 | tf_op jit(solution)/shard_map/ppermute | solution.py:465
  417.0 108.0 %factor.1 = f32[512,512]{1,0:T(8,128)} custom-call(s32[3]{0:T(128)} %pad_add_fusion.place_ref.me_ref, s32[8]{0:T(128)} %stack.153.order_ref, s32[344]{0:T(512)} %constant.28.table_ref, f32[96,256]{1,0:T(8,128)} %copy-done.23, f32[96,256]{1,0:T(8,128)} %copy-done.37, f32[96,256]{1,0:T(8,128)} %copy-done.36, f32[96,256]{1,0:T(8,128)} %copy-done.38, ...), custom_call_target="tpu_custom_call" | custom-call | flops 60000002048 | bytes 20000000 | tf_op jit(solution)/shard_map/factor/pallas_call | solution.py:202
  (242 shorter events, 169.9 us)
Async XLA Ops:
  0.0 25.2 %collective-permute-start.17 = (f32[512,512]{1,0:T(8,128)}, f32[512,512]{1,0:T(8,128)S(1)}, u32[]{:S(2)}, u32[]{:S(2)}) collective-permute-start(f32[512,512]{1,0:T(8,128)} %refs_14_.1), channel_id=1, source_target_pairs={{0,6},{2,4},{4,2},{6,0},{1,7},{3,5},{5,3},{7,1},{8,14},{10,12},{12... | collective-permute-start | bytes 3145736 | tf_op jit(solution)/shard_map/ppermute | solution.py:465
  2.2 46.6 %collective-permute-start.15 = (f32[512,512]{1,0:T(8,128)}, f32[512,512]{1,0:T(8,128)}, u32[]{:S(2)}, u32[]{:S(2)}) collective-permute-start(f32[512,512]{1,0:T(8,128)} %refs_14_.1), channel_id=1, source_target_pairs={{0,4},{2,6},{4,0},{6,2},{1,5},{3,7},{5,1},{7,3},{8,12},{10,14},{12... | collective-permute-start | bytes 3145736 | tf_op jit(solution)/shard_map/ppermute | solution.py:465
  2.4 48.5 %collective-permute-start.13 = (f32[512,512]{1,0:T(8,128)}, f32[512,512]{1,0:T(8,128)}, u32[]{:S(2)}, u32[]{:S(2)}) collective-permute-start(f32[512,512]{1,0:T(8,128)} %refs_14_.1), channel_id=1, source_target_pairs={{0,2},{2,0},{4,6},{6,4},{1,3},{3,1},{5,7},{7,5},{8,10},{10,8},{12,... | collective-permute-start | bytes 3145736 | tf_op jit(solution)/shard_map/ppermute | solution.py:465
  2.7 49.6 %collective-permute-start.12 = (f32[512,512]{1,0:T(8,128)}, f32[512,512]{1,0:T(8,128)}, u32[]{:S(2)}, u32[]{:S(2)}) collective-permute-start(f32[512,512]{1,0:T(8,128)} %refs_14_.1), channel_id=1, source_target_pairs={{0,1},{1,0},{2,3},{3,2},{4,5},{5,4},{6,7},{7,6},{8,9},{9,8},{10,11... | collective-permute-start | bytes 3145736 | tf_op jit(solution)/shard_map/ppermute | solution.py:465
  5.9 47.2 %collective-permute-start.3 = (f32[512,512]{1,0:T(8,128)S(1)}, f32[512,512]{1,0:T(8,128)S(1)}, u32[]{:S(2)}, u32[]{:S(2)}) collective-permute-start(f32[512,512]{1,0:T(8,128)S(1)} %get-tuple-element.33.refs_1_), channel_id=1, source_target_pairs={{8,0},{16,8},{24,16},{9,1},{17,9},{25,17},{10,2},{18,10},{26,18},{... | collective-permute-start | bytes 3145736 | tf_op jit(solution)/shard_map/ppermute | solution.py:493
  25.2 28.0 %collective-permute-start.1 = (f32[512,512]{1,0:T(8,128)S(1)}, f32[512,512]{1,0:T(8,128)S(1)}, u32[]{:S(2)}, u32[]{:S(2)}) collective-permute-start(f32[512,512]{1,0:T(8,128)S(1)} %get-tuple-element.33.refs_1_), channel_id=1, source_target_pairs={{0,8},{8,16},{16,24},{1,9},{9,17},{17,25},{2,10},{10,18},{18,26},{... | collective-permute-start | bytes 3145736 | tf_op jit(solution)/shard_map/ppermute | solution.py:493
  50.9 25.8 %collective-permute-start = (f32[512,512]{1,0:T(8,128)S(1)}, f32[512,512]{1,0:T(8,128)S(1)}, u32[]{:S(2)}, u32[]{:S(2)}) collective-permute-start(f32[512,512]{1,0:T(8,128)S(1)} %get-tuple-element.34.refs_0_), channel_id=1, source_target_pairs={{0,8},{8,16},{16,24},{1,9},{9,17},{17,25},{2,10},{10,18},{18,26},{... | collective-permute-start | bytes 3145736 | tf_op jit(solution)/shard_map/ppermute | solution.py:493
  52.2 27.6 %collective-permute-start.18 = (f32[512,512]{1,0:T(8,128)S(1)}, f32[512,512]{1,0:T(8,128)S(1)}, u32[]{:S(2)}, u32[]{:S(2)}) collective-permute-start(f32[512,512]{1,0:T(8,128)S(1)} %collective-permute-done.17.refs_16_.refs_20_), channel_id=1, source_target_pairs={{0,1},{1,0},{2,3},{3,2},{4,5},{5,4},{6,7},{7,6},{8,9},{9,8},{10,11... | collective-permute-start | bytes 3145736 | tf_op jit(solution)/shard_map/ppermute | solution.py:465
  53.1 28.1 %collective-permute-start.16 = (f32[512,512]{1,0:T(8,128)}, f32[512,512]{1,0:T(8,128)S(1)}, u32[]{:S(2)}, u32[]{:S(2)}) collective-permute-start(f32[512,512]{1,0:T(8,128)} %collective-permute-done.15.refs_14_.refs_18_), channel_id=1, source_target_pairs={{0,1},{1,0},{2,3},{3,2},{4,5},{5,4},{6,7},{7,6},{8,9},{9,8},{10,11... | collective-permute-start | bytes 3145736 | tf_op jit(solution)/shard_map/ppermute | solution.py:465
  53.2 42.1 %collective-permute-start.7 = (f32[512,512]{1,0:T(8,128)S(1)}, f32[512,512]{1,0:T(8,128)}, u32[]{:S(2)}, u32[]{:S(2)}) collective-permute-start(f32[512,512]{1,0:T(8,128)S(1)} %collective-permute-done.3.refs_5_), channel_id=1, source_target_pairs={{8,0},{16,8},{24,16},{9,1},{17,9},{25,17},{10,2},{18,10},{26,18},{... | collective-permute-start | bytes 3145736 | tf_op jit(solution)/shard_map/ppermute | solution.py:493
  72.8 27.6 %collective-permute-start.5 = (f32[512,512]{1,0:T(8,128)S(1)}, f32[512,512]{1,0:T(8,128)}, u32[]{:S(2)}, u32[]{:S(2)}) collective-permute-start(f32[512,512]{1,0:T(8,128)S(1)} %collective-permute-done.1.refs_3_), channel_id=1, source_target_pairs={{0,8},{8,16},{16,24},{1,9},{9,17},{17,25},{2,10},{10,18},{18,26},{... | collective-permute-start | bytes 3145736 | tf_op jit(solution)/shard_map/ppermute | solution.py:493
  76.8 41.0 %collective-permute-start.6 = (f32[512,512]{1,0:T(8,128)S(1)}, f32[512,512]{1,0:T(8,128)}, u32[]{:S(2)}, u32[]{:S(2)}) collective-permute-start(f32[512,512]{1,0:T(8,128)S(1)} %collective-permute-done.2.refs_4_), channel_id=1, source_target_pairs={{8,0},{16,8},{24,16},{9,1},{17,9},{25,17},{10,2},{18,10},{26,18},{... | collective-permute-start | bytes 3145736 | tf_op jit(solution)/shard_map/ppermute | solution.py:493
  79.9 43.2 %collective-permute-start.4 = (f32[512,512]{1,0:T(8,128)S(1)}, f32[512,512]{1,0:T(8,128)}, u32[]{:S(2)}, u32[]{:S(2)}) collective-permute-start(f32[512,512]{1,0:T(8,128)S(1)} %collective-permute-done.refs_2_), channel_id=1, source_target_pairs={{0,8},{8,16},{16,24},{1,9},{9,17},{17,25},{2,10},{10,18},{18,26},{... | collective-permute-start | bytes 3145736 | tf_op jit(solution)/shard_map/ppermute | solution.py:493
  81.2 44.5 %collective-permute-start.14 = (f32[512,512]{1,0:T(8,128)}, f32[512,512]{1,0:T(8,128)}, u32[]{:S(2)}, u32[]{:S(2)}) collective-permute-start(f32[512,512]{1,0:T(8,128)} %collective-permute-done.13.refs_12_.refs_16_), channel_id=1, source_target_pairs={{0,1},{1,0},{2,3},{3,2},{4,5},{5,4},{6,7},{7,6},{8,9},{9,8},{10,11... | collective-permute-start | bytes 3145736 | tf_op jit(solution)/shard_map/ppermute | solution.py:465
  95.3 45.0 %collective-permute-start.11 = (f32[512,512]{1,0:T(8,128)}, f32[512,512]{1,0:T(8,128)}, u32[]{:S(2)}, u32[]{:S(2)}) collective-permute-start(f32[512,512]{1,0:T(8,128)} %collective-permute-done.7.refs_9_), channel_id=1, source_target_pairs={{8,0},{16,8},{24,16},{9,1},{17,9},{25,17},{10,2},{18,10},{26,18},{... | collective-permute-start | bytes 3145736 | tf_op jit(solution)/shard_map/ppermute | solution.py:493
  100.5 42.7 %collective-permute-start.9 = (f32[512,512]{1,0:T(8,128)}, f32[512,512]{1,0:T(8,128)}, u32[]{:S(2)}, u32[]{:S(2)}) collective-permute-start(f32[512,512]{1,0:T(8,128)} %collective-permute-done.5.refs_7_), channel_id=1, source_target_pairs={{0,8},{8,16},{16,24},{1,9},{9,17},{17,25},{2,10},{10,18},{18,26},{... | collective-permute-start | bytes 3145736 | tf_op jit(solution)/shard_map/ppermute | solution.py:493
  117.8 45.0 %collective-permute-start.10 = (f32[512,512]{1,0:T(8,128)}, f32[512,512]{1,0:T(8,128)}, u32[]{:S(2)}, u32[]{:S(2)}) collective-permute-start(f32[512,512]{1,0:T(8,128)} %collective-permute-done.6.refs_8_), channel_id=1, source_target_pairs={{8,0},{16,8},{24,16},{9,1},{17,9},{25,17},{10,2},{18,10},{26,18},{... | collective-permute-start | bytes 3145736 | tf_op jit(solution)/shard_map/ppermute | solution.py:493
  123.1 42.6 %collective-permute-start.8 = (f32[512,512]{1,0:T(8,128)}, f32[512,512]{1,0:T(8,128)}, u32[]{:S(2)}, u32[]{:S(2)}) collective-permute-start(f32[512,512]{1,0:T(8,128)} %collective-permute-done.4.refs_6_), channel_id=1, source_target_pairs={{0,8},{8,16},{16,24},{1,9},{9,17},{17,25},{2,10},{10,18},{18,26},{... | collective-permute-start | bytes 3145736 | tf_op jit(solution)/shard_map/ppermute | solution.py:493
  227.2 26.0 %collective-permute-start.45 = (f32[512,256]{1,0:T(8,128)S(1)}, f32[512,256]{1,0:T(8,128)S(1)}, u32[]{:S(2)}, u32[]{:S(2)}) collective-permute-start(f32[512,256]{1,0:T(8,128)S(1)} %collective-permute-done.35.refs_2_.refs_27_), channel_id=1, source_target_pairs={{0,8},{8,16},{16,24},{1,9},{9,17},{17,25},{2,10},{10,18},{18,26},{... | collective-permute-start | bytes 1572872 | tf_op jit(solution)/shard_map/ppermute | solution.py:533
  246.5 36.5 %collective-permute-start.37 = (f32[4,224,256]{2,1,0:T(8,128)S(1)}, f32[4,224,256]{2,1,0:T(8,128)S(1)}, u32[]{:S(2)}, u32[]{:S(2)}) collective-permute-start(f32[4,224,256]{2,1,0:T(8,128)S(1)} %get-tuple-element.26), channel_id=1, source_target_pairs={{0,1},{1,0},{2,3},{3,2},{4,5},{5,4},{6,7},{7,6},{8,9},{9,8},{10,11... | collective-permute-start | bytes 2752520 | tf_op jit(solution)/shard_map/ppermute | solution.py:465
  253.2 30.0 %collective-permute-start.55 = (f32[512,256]{1,0:T(8,128)S(1)}, f32[512,256]{1,0:T(8,128)S(1)}, u32[]{:S(2)}, u32[]{:S(2)}) collective-permute-start(f32[512,256]{1,0:T(8,128)S(1)} %collective-permute-done.45.refs_4_.refs_29_), channel_id=1, source_target_pairs={{0,8},{8,16},{16,24},{1,9},{9,17},{17,25},{2,10},{10,18},{18,26},{... | collective-permute-start | bytes 1572872 | tf_op jit(solution)/shard_map/ppermute | solution.py:533
  270.9 40.3 %collective-permute-start.47 = (f32[4,352,256]{2,1,0:T(8,128)S(1)}, f32[4,352,256]{2,1,0:T(8,128)S(1)}, u32[]{:S(2)}, u32[]{:S(2)}) collective-permute-start(f32[4,352,256]{2,1,0:T(8,128)S(1)} %get-tuple-element.28), channel_id=1, source_target_pairs={{0,1},{1,0},{2,3},{3,2},{4,5},{5,4},{6,7},{7,6},{8,9},{9,8},{10,11... | collective-permute-start | bytes 4325384 | tf_op jit(solution)/shard_map/ppermute | solution.py:465
  305.2 29.0 %collective-permute-start.38 = (f32[224,256]{1,0:T(8,128)S(1)}, f32[224,256]{1,0:T(8,128)S(1)}, u32[]{:S(2)}, u32[]{:S(2)}) collective-permute-start(f32[224,256]{1,0:T(8,128)S(1)} %get-tuple-element.48), channel_id=1, source_target_pairs={{0,2},{2,0},{4,6},{6,4},{1,3},{3,1},{5,7},{7,5},{8,10},{10,8},{12,... | collective-permute-start | bytes 688136 | tf_op jit(solution)/shard_map/ppermute | solution.py:465
  388.3 28.7 %collective-permute-start.54 = (f32[4,352,256]{2,1,0:T(8,128)S(1)}, f32[4,352,256]{2,1,0:T(8,128)}, u32[]{:S(2)}, u32[]{:S(2)}) collective-permute-start(f32[4,352,256]{2,1,0:T(8,128)S(1)} %pad_maximum_fusion), channel_id=1, source_target_pairs={{0,1},{1,0},{2,3},{3,2},{4,5},{5,4},{6,7},{7,6},{8,9},{9,8},{10,11... | collective-permute-start | bytes 4325384 | tf_op jit(solution)/shard_map/ppermute | solution.py:465
  (88 other events, 2079.3 us)
